TPU v7x, 32 devices: a 4x4x1 block of a 4x4x8 slice. The times are simulated.
32 devices in a mesh: part: 1 (over z), tp: 4 (over y), dp: 8 (over x, core).
Axes of the slice: x: 4, y: 4, z: 1, core: 2. Of those that a mesh axis runs over, the one named last changes fastest.
The devices are a block of a 4x4x8 slice.
Arguments:
- hidden: bfloat16 [24, 384, 5120], P(('part', 'dp'))
- ln_scale: float32 [5120], replicated
- w_q: bfloat16 [5120, 5120], P('dp', 'tp')
- w_kv: bfloat16 [5120, 256], P('dp')
- w_gate: bfloat16 [5120, 20480], P('dp', 'tp')
- w_up: bfloat16 [5120, 20480], P('dp', 'tp')
- w_o: bfloat16 [5120, 5120], P('tp', 'dp')
- w_down: bfloat16 [20480, 5120], P('tp', 'dp')
- prompt_len: int32 [24], P(('part', 'dp'))
Outputs:
- output 1: bfloat16 [24, 384, 5120], P(('part', 'dp'))
- output 2: bfloat16 [24, 384, 128], P(('part', 'dp'))
- output 3: bfloat16 [24, 384, 128], P(('part', 'dp'))
All inputs are finite; a program needn't handle non-finite values.
Results may differ from a plain program's by a relative error of at most 0.00937125.
Values are sent between devices in bfloat16 or wider.
A program may use at most 768 MiB of HBM per device.

v0:
```python
import jax
import jax.numpy as jnp
from jax import lax
from jax.sharding import PartitionSpec as P

LN_EPS = 1e-6
ROPE_BASE = 10000.0
MASK_VALUE = -1e30


def layer_norm(hidden, ln_scale):
    x_f = hidden.astype(jnp.float32)
    row_mean = jnp.mean(x_f, axis=-1, keepdims=True)
    centered = x_f - row_mean
    row_var = jnp.mean(centered * centered, axis=-1, keepdims=True)
    return (centered * lax.rsqrt(row_var + LN_EPS) * ln_scale).astype(jnp.bfloat16)


def rope_tables(seq_len, head_dim):
    half_dim = head_dim // 2
    inv_freq = ROPE_BASE ** (-2.0 * jnp.arange(half_dim, dtype=jnp.float32) / head_dim)
    angles = jnp.arange(seq_len, dtype=jnp.float32)[:, None] * inv_freq[None, :]
    return jnp.cos(angles), jnp.sin(angles)


def apply_rope(x_in, cos_tab, sin_tab):
    half_dim = x_in.shape[-1] // 2
    x_lo = x_in[..., :half_dim]
    x_hi = x_in[..., half_dim:]
    return jnp.concatenate([x_lo * cos_tab - x_hi * sin_tab, x_hi * cos_tab + x_lo * sin_tab], axis=-1)


def attend_and_gate(z_all, prompt_len, head_dim, ff_width):
    n_seq, seq_len, z_cols = z_all.shape
    q_width = z_cols - 2 * head_dim - 2 * ff_width
    n_heads = q_width // head_dim
    gate_start = q_width + 2 * head_dim
    cos_tab, sin_tab = rope_tables(seq_len, head_dim)
    q_heads = z_all[:, :, :q_width].reshape(n_seq, seq_len, n_heads, head_dim).astype(jnp.float32)
    q_rot = apply_rope(q_heads, cos_tab[:, None, :], sin_tab[:, None, :]).astype(jnp.bfloat16)
    k_rot = apply_rope(z_all[:, :, q_width:q_width + head_dim].astype(jnp.float32), cos_tab, sin_tab).astype(jnp.bfloat16)
    v_val = z_all[:, :, q_width + head_dim:gate_start]
    gate_lin = z_all[:, :, gate_start:gate_start + ff_width]
    up_lin = z_all[:, :, gate_start + ff_width:]
    scores = jnp.einsum('crie,cle->cirl', q_rot, k_rot, preferred_element_type=jnp.float32) * (head_dim ** -0.5)
    positions = jnp.arange(seq_len)
    causal = positions[None, :] <= positions[:, None]
    key_live = positions[None, :] < prompt_len[:, None]
    key_mask = causal[None, None, :, :] & key_live[:, None, None, :]
    probs_bf = jax.nn.softmax(jnp.where(key_mask, scores, MASK_VALUE), axis=-1).astype(jnp.bfloat16)
    attn_out = jnp.einsum('cirl,cle->crie', probs_bf, v_val, preferred_element_type=jnp.float32).astype(jnp.bfloat16)
    ffn_act = (jax.nn.silu(gate_lin.astype(jnp.float32)) * up_lin.astype(jnp.float32)).astype(jnp.bfloat16)
    mixed = jnp.concatenate([attn_out.reshape(n_seq, seq_len, q_width), ffn_act], axis=-1)
    return mixed, k_rot, v_val


def solution(mesh):
    batch_spec = P(('part', 'dp'), None, None)

    def local_layer(hidden, ln_scale, w_q, w_kv, w_gate, w_up, w_o, w_down, prompt_len):
        head_dim = w_kv.shape[1] // 2
        ff_width = w_gate.shape[1]
        w_in_blk = jnp.concatenate([w_q, w_kv, w_gate, w_up], axis=1)
        w_out_blk = jnp.concatenate([w_o, w_down], axis=0)
        w_in_full = lax.all_gather(w_in_blk, 'dp', axis=0, tiled=True)
        w_out_full = lax.all_gather(w_out_blk, 'dp', axis=1, tiled=True)
        normed = layer_norm(hidden, ln_scale)
        z_all = jnp.einsum('bld,de->ble', normed, w_in_full, preferred_element_type=jnp.float32).astype(jnp.bfloat16)
        mixed, k_rot, v_val = attend_and_gate(z_all, prompt_len, head_dim, ff_width)
        y_part = jnp.einsum('ble,ed->bld', mixed, w_out_full, preferred_element_type=jnp.float32).astype(jnp.bfloat16)
        y_sum = lax.psum(y_part, 'tp')
        out = (hidden.astype(jnp.float32) + y_sum.astype(jnp.float32)).astype(jnp.bfloat16)
        return out, k_rot, v_val

    return jax.shard_map(
        local_layer,
        mesh=mesh,
        in_specs=(batch_spec, P(None), P('dp', 'tp'), P('dp', None), P('dp', 'tp'), P('dp', 'tp'), P('tp', 'dp'), P('tp', 'dp'), P(('part', 'dp'))),
        out_specs=(batch_spec, batch_spec, batch_spec),
        check_vma=False,
    )
```

profile of v0, /device:TPU:97, one launch (start us, length us, event | category | flops | bytes accessed | tf_op | source)
XLA Modules:
  0.0 1149.2 jit_solution(5786954851255076029)
XLA Ops:
  7.2 0.1 all-gather.3.cloned.1.call-start
  7.2 12.5 %pad_maximum_fusion = bf16[640,11776]{1,0:T(8,128)(2,1)} fusion(bf16[640,5120]{1,0:T(8,128)(2,1)} %param.14, bf16[640,5120]{1,0:T(8,128)(2,1)} %param.13, bf16[640,256]{1,0:T(8,128)(2,1)} %param.12, bf16[640,1280]{1,0:T(8,128)(2,1)} %param.11), kind=kLoop, calls=%fused_computation.25 | loop fusion | flops 60293120 | bytes 30146560 | tf_op jit(solution)/shard_map/concatenate | solution.py:63
  19.7 0.1 all-gather.3.cloned.1.call-update
  19.8 0.1 all-gather.5.cloned.1.call-start
  19.9 1.3 copy-done.2
  21.2 6.8 pad_maximum_fusion.1
  28.1 0.1 all-reduce.2.cloned.1.call-start
  28.2 0.1 iota_compare_fusion.1
  28.3 6.0 convert_reduce_fusion
  34.3 7.5 fusion.10
  41.8 1.5 fusion.44
  43.3 1.0 broadcast_and_fusion
  44.3 500.1 %all-gather.3.cloned.1.call-done = bf16[5120,11776]{1,0:T(8,128)(2,1)} async-done(((bf16[640,11776]{1,0:T(8,128)(2,1)}), bf16[5120,11776]{1,0:T(8,128)(2,1)}) %all-gather.3.cloned.1.call-update) | async-done | bytes 120586256 | tf_op jit(solution)/shard_map/all_gather | solution.py:65
  544.4 155.7 %fusion.7 = bf16[3,384,11776]{2,1,0:T(8,128)(2,1)} fusion(bf16[5120,11776]{1,0:T(8,128)(2,1)} %all-gather.3.cloned.1.call-done, bf16[3,384,5120]{2,1,0:T(8,128)(2,1)} %param.9, f32[5120]{0:T(1024)S(1)} %copy-done.7, f32[3,384]{1,0:T(4,128)S(1)} %add_rsqrt_fusion, f32[3,384]{1,0:T(4,128)S(1)} %broadcast_multiply_fusion), kind=kOutput, calls=%fused_computation.12 | convolution fusion | flops 138958405632 | bytes 159544320 | tf_op jit(solution)/shard_map/bld,de->ble/dot_general | solution.py:68
  700.0 4.9 slice_convert_fusion
  704.9 7.7 copy.17
  712.6 4.9 fusion.50
  717.5 5.5 copy.28
  723.1 3.8 copy.29
  726.9 1.1 fusion.49
  728.1 0.3 subtract_convert_fusion.1
  728.3 0.2 pad_maximum_fusion.2
  728.5 5.6 subtract_convert_fusion
  734.2 8.6 fusion.36
  742.8 18.3 %fusion.51 = (f32[3,10,384]{2,1,0:T(8,128)S(1)}, f32[3,10,384,384]{2,3,1,0:T(8,128)}) fusion(f32[3,384,384,10]{2,1,3,0:T(8,128)} %fusion.36, pred[3,384,384]{1,2,0:T(8,128)(4,1)S(1)} %copy-done.4), kind=kOutput, calls=%fused_computation.68 | output fusion | flops 26542464 | bytes 35877888 | tf_op jit(solution)/shard_map/sub | solution.py:50
  761.2 9.5 fusion.40
  770.7 4.0 copy.22
  774.7 15.6 %fusion.18 = bf16[3,384,5120]{2,1,0:T(8,128)(2,1)} fusion(bf16[3,384,11776]{2,1,0:T(8,128)(2,1)} %fusion.7), kind=kLoop, calls=%fused_computation.21 | loop fusion | flops 47185920 | bytes 35389440 | tf_op jit(solution)/shard_map/convert_element_type | solution.py:52
  790.2 42.5 %all-gather.5.cloned.1.call-done = bf16[6400,5120]{1,0:T(8,128)(2,1)} async-done(((bf16[6400,640]{1,0:T(8,128)(2,1)}), bf16[6400,5120]{1,0:T(8,128)(2,1)}) %all-gather.5.cloned.1.call-update) | async-done | bytes 65536016 | tf_op jit(solution)/shard_map/all_gather | solution.py:66
  832.7 85.9 %fusion.27 = bf16[3,384,5120]{2,1,0:T(8,128)(2,1)} fusion(bf16[6400,5120]{1,0:T(8,128)(2,1)} %all-gather.5.cloned.1.call-done, bf16[3,384,5120]{2,1,0:T(8,128)(2,1)} %fusion.18, bf16[3,384,1280]{2,1,0:T(8,128)(2,1)S(1)} %copy.22), kind=kOutput, calls=%fused_computation.33 | convolution fusion | flops 75532861440 | bytes 92078080 | tf_op jit(solution)/shard_map/ble,ed->bld/dot_general | solution.py:70
  918.7 210.1 %all-reduce.2.cloned.1.call-done = bf16[3,384,5120]{2,1,0:T(8,128)(2,1)} async-done(((bf16[3,384,5120]{2,1,0:T(8,128)(2,1)}), bf16[3,384,5120]{2,1,0:T(8,128)(2,1)}) %all-reduce.2.cloned.1.call-update) | async-done | bytes 11796496 | tf_op jit(solution)/shard_map/psum | solution.py:71
  1128.8 13.8 %fusion.17 = bf16[3,384,5120]{2,1,0:T(8,128)(2,1)} fusion(bf16[3,384,5120]{2,1,0:T(8,128)(2,1)} %param.9, bf16[3,384,5120]{2,1,0:T(8,128)(2,1)} %all-reduce.2.cloned.1.call-done), kind=kLoop, calls=%fused_computation.20 | loop fusion | flops 23592960 | bytes 35389440 | tf_op jit(solution)/shard_map/convert_element_type | solution.py:72
  (21 shorter events, 0.2 us)
Async XLA Ops:
  7.2 537.2 %all-gather.3.cloned.1.call-start = ((), (), s32[]{:S(2)}) async-start(), calls=%async_computation | async-start | bytes 135659520 | tf_op jit(solution)/shard_map/all_gather | solution.py:65
  19.7 1.4 copy-start.2
  19.8 8.4 copy-start.6
  19.8 812.9 %all-gather.5.cloned.1.call-start = ((), (), s32[]{:S(2)}) async-start(), calls=%async_computation.1 | async-start | bytes 73728000 | tf_op jit(solution)/shard_map/all_gather | solution.py:66
  28.0 516.4 %copy-start.7 = (f32[5120]{0:T(1024)S(1)}, f32[5120]{0:T(1024)}, u32[]{:S(2)}) copy-start(f32[5120]{0:T(1024)} %param.10) | copy-start | bytes 61444
  28.1 1100.7 %all-reduce.2.cloned.1.call-start = ((), (), s32[]{:S(2)}) async-start(), calls=%async_computation.2 | async-start | bytes 23592960 | tf_op jit(solution)/shard_map/psum | solution.py:71
  712.6 15.4 %copy-start = (f32[384,64]{1,0:T(8,128)S(1)}, f32[384,64]{1,0:T(8,128)}, u32[]{:S(2)}) copy-start(f32[384,64]{1,0:T(8,128)} %get-tuple-element.11) | copy-start | bytes 294916
  712.6 15.4 %copy-start.1 = (f32[384,64]{1,0:T(8,128)S(1)}, f32[384,64]{1,0:T(8,128)}, u32[]{:S(2)}) copy-start(f32[384,64]{1,0:T(8,128)} %get-tuple-element.12) | copy-start | bytes 294916
  728.0 33.1 %copy-start.5 = (bf16[3,384,128]{2,1,0:T(8,128)(2,1)}, bf16[3,384,128]{2,1,0:T(8,128)(2,1)S(1)}, u32[]{:S(2)}) copy-start(bf16[3,384,128]{2,1,0:T(8,128)(2,1)S(1)} %get-tuple-element.3) | copy-start | bytes 884740
  728.5 5.7 copy-start.3
  734.2 8.7 copy-start.4
Sparse Core Ops, SparseCore 0:
  19.9 524.4 all-gather.2
  546.0 286.6 all-gather.4
  918.8 209.9 all-reduce.1
where the time goes:
time: 1150 us
  waiting for transfers between devices  753 us (65%)
  matrix products  260 us (23%)
  other arithmetic  95.3 us (8%)
  local copies, waits for them, and re-layouts  27.2 us (2%)
  between operations  13.9 us (1%)
    all_gather x1, waiting for transfers between devices, local_layer(): w_in_full = lax.all_gather(w_in_blk, 'dp', axis=0, tiled=True)  500 us
    psum x1, waiting for transfers between devices, local_layer(): y_sum = lax.psum(y_part, 'tp')  210 us
    dot_general x1, matrix products, local_layer(): jnp.einsum('bld,de->ble', normed, w_in_full, preferred_element_type=jnp.f...  156 us
    dot_general x1, matrix products, local_layer(): jnp.einsum('ble,ed->bld', mixed, w_out_full, preferred_element_type=jnp.f...  85.9 us
    all_gather x1, waiting for transfers between devices, local_layer(): w_out_full = lax.all_gather(w_out_blk, 'dp', axis=1, tiled=True)  42.5 us
  transfers between devices with their start and end apart: 3, of which 3 were waited for; matrix products, arithmetic and copies ran while one was open for 23% of the time, Pallas kernels for 0%

commit v1 on v0

v1 whole, which is shorter than its diff:
```python
import functools

import jax
import jax.numpy as jnp
from jax import lax
from jax.experimental import pallas as pl
from jax.experimental.pallas import tpu as pltpu
from jax.sharding import PartitionSpec as P


LN_EPS = 1e-6
ROPE_BASE = 10000.0
MASK_VALUE = -1e30
VMEM_LIMIT = 60 * 1024 * 1024


SIB, PAIR, CUT = 1, 2, 6
OWNERS = (0, PAIR, CUT, CUT ^ PAIR)


def cost(flops, nbytes):
    return pl.CostEstimate(flops=int(flops), bytes_accessed=int(nbytes), transcendentals=0)


def ln_kernel(h_ref, s_ref, u_ref):
    x_f = h_ref[...].astype(jnp.float32)
    row_mean = jnp.mean(x_f, axis=-1, keepdims=True)
    centered = x_f - row_mean
    row_var = jnp.mean(centered * centered, axis=-1, keepdims=True)
    u_ref[...] = (centered * lax.rsqrt(row_var + LN_EPS) * s_ref[...]).astype(jnp.bfloat16)


def layer_norm(h, ln_scale):
    rows, width = h.shape
    tile = 96
    return pl.pallas_call(
        ln_kernel,
        grid=(rows // tile,),
        in_specs=[pl.BlockSpec((tile, width), lambda i: (i, 0)), pl.BlockSpec((1, width), lambda i: (0, 0))],
        out_specs=pl.BlockSpec((tile, width), lambda i: (i, 0)),
        out_shape=jax.ShapeDtypeStruct((rows, width), jnp.bfloat16),
        cost_estimate=cost(8 * rows * width, 4 * rows * width),
        name="norm",
    )(h, ln_scale.reshape(1, width))


def load_rows(dp_ref, blocks, wbuf, sem):
    depth = blocks[0].shape[0]
    copies = []
    for j, mask in enumerate(m ^ c for m in OWNERS for c in (0, SIB)):
        start = pl.multiple_of((dp_ref[0] ^ mask) * depth, depth)
        copies.append(pltpu.make_async_copy(blocks[j], wbuf.at[pl.ds(start, depth), :], sem.at[j]))
    for c in copies:
        c.start()
    for c in copies:
        c.wait()


def qkv_kernel(head_dim, seq_len, dp_ref, len_ref, u_ref, cos_ref, sin_ref, *refs):
    blocks, (o_ref, k_ref, v_ref, wbuf, sem) = refs[:8], refs[-5:]

    @pl.when(pl.program_id(0) == 0)
    def _():
        load_rows(dp_ref, blocks, wbuf, sem)

    n_valid = len_ref[pl.program_id(0)]
    half = head_dim // 2
    q_width = wbuf.shape[1] - 2 * head_dim
    z = jnp.dot(u_ref[...], wbuf[...], preferred_element_type=jnp.float32).astype(jnp.bfloat16)
    cos_t, sin_t = cos_ref[...], sin_ref[...]

    def rope(x_bf):
        x = x_bf.astype(jnp.float32)
        return (x * cos_t + pltpu.roll(x, half, 1) * sin_t).astype(jnp.bfloat16)

    k_rot = rope(z[:, q_width:q_width + head_dim])
    v_val = z[:, q_width + head_dim:]
    k_ref[...] = k_rot
    v_ref[...] = v_val
    rows = lax.broadcasted_iota(jnp.int32, (seq_len, seq_len), 0)
    cols = lax.broadcasted_iota(jnp.int32, (seq_len, seq_len), 1)
    live = (cols <= rows) & (cols < n_valid)
    for h in range(q_width // head_dim):
        q_rot = rope(z[:, h * head_dim:(h + 1) * head_dim])
        s = lax.dot_general(q_rot, k_rot, (((1,), (1,)), ((), ())), preferred_element_type=jnp.float32)
        s = jnp.where(live, s * (head_dim ** -0.5), MASK_VALUE)
        e = jnp.exp(s - jnp.max(s, axis=-1, keepdims=True))
        p = (e * (1.0 / jnp.sum(e, axis=-1, keepdims=True))).astype(jnp.bfloat16)
        o = jnp.dot(p, v_val, preferred_element_type=jnp.float32)
        o_ref[:, h * head_dim:(h + 1) * head_dim] = o.astype(jnp.bfloat16)


def qkv_attend(dp, lens, u, cos_t, sin_t, blocks, head_dim, seq_len, mixed_width, mixed=None):
    rows, width = u.shape
    _, cols = blocks[0].shape
    q_width = cols - 2 * head_dim
    whole = lambda shape: pl.BlockSpec(shape, lambda i: (0, 0))
    smem = pl.BlockSpec(memory_space=pltpu.SMEM)
    later = mixed is not None
    first = rows // seq_len if later else 0
    return pl.pallas_call(
        functools.partial(qkv_kernel, head_dim, seq_len),
        grid=(rows // seq_len,),
        in_specs=[smem, smem, pl.BlockSpec((seq_len, width), lambda i: (i, 0)),
                  whole((seq_len, head_dim)), whole((seq_len, head_dim))] + [pl.BlockSpec(memory_space=pl.ANY)] * (8 + later),
        out_specs=[pl.BlockSpec((seq_len, q_width), lambda i: (first + i, 0)),
                   pl.BlockSpec((seq_len, head_dim), lambda i: (i, 0)),
                   pl.BlockSpec((seq_len, head_dim), lambda i: (i, 0))],
        out_shape=[jax.ShapeDtypeStruct((2 * rows, mixed_width), jnp.bfloat16),
                   jax.ShapeDtypeStruct((rows, head_dim), jnp.bfloat16),
                   jax.ShapeDtypeStruct((rows, head_dim), jnp.bfloat16)],
        scratch_shapes=[pltpu.VMEM((width, cols), jnp.bfloat16), pltpu.SemaphoreType.DMA((8,))],
        input_output_aliases={13: 0} if later else {},
        compiler_params=pltpu.CompilerParams(vmem_limit_bytes=VMEM_LIMIT),
        cost_estimate=cost(2 * rows * width * cols * 2, 2 * (rows * width + width * cols)),
        name="qkv",
    )(dp, lens, u, cos_t, sin_t, *blocks, *([mixed] if later else []))


def ffn_kernel(steps, dp_ref, u0, u1, *refs):
    blocks, (_, a_ref, wbuf, ubuf, sem, usem) = refs[:8], refs[8:]
    i = pl.program_id(0)
    tile = ubuf.shape[1]

    def fetch(step):
        row = pl.multiple_of(lax.rem(step, steps) * tile, tile)
        slot = lax.rem(step, 2)
        for j, u in enumerate((u0, u1)):
            @pl.when(step // steps == j)
            def _(u=u):
                pltpu.make_async_copy(u.at[pl.ds(row, tile), :], ubuf.at[slot], usem.at[slot]).start()

    @pl.when(i == 0)
    def _():
        fetch(i)
        load_rows(dp_ref, blocks, wbuf, sem)

    @pl.when(i + 1 < 2 * steps)
    def _():
        fetch(i + 1)

    slot = lax.rem(i, 2)
    pltpu.make_async_copy(u0.at[pl.ds(0, tile), :], ubuf.at[slot], usem.at[slot]).wait()
    n = a_ref.shape[1]
    z = jnp.dot(ubuf[slot], wbuf[...], preferred_element_type=jnp.float32).astype(jnp.bfloat16)
    g, p = z[:, :n].astype(jnp.float32), z[:, n:].astype(jnp.float32)
    a_ref[...] = (g * jax.nn.sigmoid(g) * p).astype(jnp.bfloat16)


def ffn_chunk(dp, u_own, u_pair, blocks, mixed, place):
    rows, width = u_own.shape
    cols = blocks[0].shape[1]
    steps = 2
    tile, n = rows // steps, cols // 2
    anywhere = pl.BlockSpec(memory_space=pl.ANY)
    return pl.pallas_call(
        functools.partial(ffn_kernel, steps),
        grid=(2 * steps,),
        in_specs=[pl.BlockSpec(memory_space=pltpu.SMEM)] + [anywhere] * 11,
        out_specs=pl.BlockSpec((tile, n), lambda i: (i, place)),
        out_shape=jax.ShapeDtypeStruct(mixed.shape, mixed.dtype),
        scratch_shapes=[pltpu.VMEM((width, cols), jnp.bfloat16), pltpu.VMEM((2, tile, width), jnp.bfloat16),
                        pltpu.SemaphoreType.DMA((8,)), pltpu.SemaphoreType.DMA((2,))],
        input_output_aliases={11: 0},
        compiler_params=pltpu.CompilerParams(vmem_limit_bytes=VMEM_LIMIT),
        cost_estimate=cost(4 * rows * width * cols, 2 * (2 * rows * width + width * cols)),
        name="ffn",
    )(dp, u_own, u_pair, *blocks, mixed)


def down_kernel(steps, joint, core_ref, x_ref, w0, w1, *refs):
    both_ref, solo_ref, wbuf, sem = refs[-4:]
    i = pl.program_id(0)

    @pl.when(i == 0)
    def _():
        n = w0.shape[1]
        copies = []
        for j, w in enumerate((w0, w1)):
            start = pl.multiple_of((core_ref[0] ^ j) * n, n)
            copies.append(pltpu.make_async_copy(w, wbuf.at[:, pl.ds(start, n)], sem.at[j]))
        for c in copies:
            c.start()
        for c in copies:
            c.wait()

    y = jnp.dot(x_ref[...], wbuf[...], preferred_element_type=jnp.float32).astype(jnp.bfloat16)

    @pl.when(i // steps == joint)
    def _():
        both_ref[...] = y

    @pl.when(i // steps != joint)
    def _():
        solo_ref[...] = y


def down_block(core, mixed, w0, w1, both=None):
    depth = mixed.shape[1]
    n = w0.shape[1]
    rows, steps = mixed.shape[0] // 2, 2
    tile = rows // steps
    joint = 0 if both is None else 1
    first = joint * steps
    anywhere = pl.BlockSpec(memory_space=pl.ANY)
    hold = lambda i, start: jnp.clip(i - start, 0, steps - 1)
    return pl.pallas_call(
        functools.partial(down_kernel, steps, joint),
        grid=(2 * steps,),
        in_specs=[pl.BlockSpec(memory_space=pltpu.SMEM), pl.BlockSpec((tile, depth), lambda i: (i, 0))]
        + [anywhere] * (2 + joint),
        out_specs=[pl.BlockSpec((tile, 2 * n), lambda i: (first + hold(i, first), 0)),
                   pl.BlockSpec((tile, 2 * n), lambda i: (hold(i, steps - first), 0))],
        out_shape=[jax.ShapeDtypeStruct((2 * rows, 2 * n), jnp.bfloat16), jax.ShapeDtypeStruct((rows, 2 * n), jnp.bfloat16)],
        scratch_shapes=[pltpu.VMEM((depth, 2 * n), jnp.bfloat16), pltpu.SemaphoreType.DMA((2,))],
        input_output_aliases={4: 0} if joint else {},
        compiler_params=pltpu.CompilerParams(vmem_limit_bytes=VMEM_LIMIT),
        cost_estimate=cost(8 * rows * depth * n, 4 * (rows * depth + depth * n + 2 * rows * n)),
        name="down",
    )(core, mixed, w0, w1, *([] if both is None else [both]))


def solution(mesh):
    n_dp, n_tp = mesh.shape['dp'], mesh.shape['tp']
    batch_spec = P(('part', 'dp'), None, None)

    def swap(x, mask):
        return lax.ppermute(x, 'dp', [(i, i ^ mask) for i in range(n_dp)])

    def local_layer(hidden, ln_scale, w_q, w_kv, w_gate, w_up, w_o, w_down, prompt_len):
        n_seq, seq_len, width = hidden.shape
        rows = n_seq * seq_len
        head_dim = w_kv.shape[1] // 2
        q_half, f_half = w_q.shape[1] // 2, w_gate.shape[1] // 2
        out_cols = w_o.shape[1]
        n_ffn = f_half // q_half
        dp, tp = lax.axis_index('dp'), lax.axis_index('tp')
        core, chip = dp % 2, dp // 2
        mine = ((chip + 1) // 2) % 2
        dp_arr, core_arr = dp.reshape(1).astype(jnp.int32), core.reshape(1).astype(jnp.int32)

        def in_chunk(k, half):
            if k == 0:
                return jnp.concatenate([lax.dynamic_slice_in_dim(w_q, half * q_half, q_half, 1), w_kv], axis=1)
            start = half * f_half + (k - 1) * q_half
            return jnp.concatenate([lax.dynamic_slice_in_dim(w_gate, start, q_half, 1),
                                    lax.dynamic_slice_in_dim(w_up, start, q_half, 1)], axis=1)

        def out_chunk(half):
            return jnp.concatenate([lax.dynamic_slice_in_dim(w_o, half * q_half, q_half, 0),
                                    lax.dynamic_slice_in_dim(w_down, half * f_half, f_half, 0)], axis=0)

        def gather(make):
            own, other = lax.optimization_barrier((make(mine), make(1 - mine)))
            cut = swap(own, CUT)
            pair = swap(other, PAIR)
            relay = swap(pair, CUT)
            blocks = []
            for b in (own, pair, cut, relay):
                blocks += [b, swap(b, SIB)]
            return blocks

        chunks = [gather(functools.partial(in_chunk, k)) for k in range(n_ffn + 1)]
        outs = gather(out_chunk)

        h_own = hidden.reshape(rows, width)
        quarter = rows // n_tp
        h_quarter = lax.dynamic_slice_in_dim(h_own, tp * quarter, quarter, 0)
        u_quarter = layer_norm(h_quarter, ln_scale)
        u_own = layer_norm(h_own, ln_scale)
        u_quarter = swap(u_quarter, PAIR)
        u_pair = lax.all_gather(u_quarter, 'tp', axis=0, tiled=True)
        len_pair = swap(prompt_len, PAIR)

        half_dim = head_dim // 2
        inv_freq = ROPE_BASE ** (-2.0 * jnp.arange(half_dim, dtype=jnp.float32) / head_dim)
        angles = jnp.arange(seq_len, dtype=jnp.float32)[:, None] * inv_freq[None, :]
        cos_t, sin_t = jnp.cos(angles), jnp.sin(angles)
        cos_t = jnp.concatenate([cos_t, cos_t], axis=1)
        sin_t = jnp.concatenate([-sin_t, sin_t], axis=1)

        mixed_width = q_half + f_half
        attend = lambda lens, u, *mixed: qkv_attend(
            dp_arr, lens, u, cos_t, sin_t, chunks[0], head_dim, seq_len, mixed_width, *mixed)
        mixed, k_rot, v_val = attend(prompt_len, u_own)
        mixed, _, _ = attend(len_pair, u_pair, mixed)
        for k in range(1, n_ffn + 1):
            mixed = ffn_chunk(dp_arr, u_own, u_pair, chunks[k], mixed, k)

        f32 = jnp.float32
        n_cols = 2 * out_cols
        out = jnp.zeros((rows, width), jnp.bfloat16)
        odd = chip % 2
        h_last = h_quarter
        for j in (0, 2):
            both, to_pair = down_block(core_arr, mixed, outs[2 * j], outs[2 * j + 1])
            both, own = down_block(core_arr, mixed, outs[2 * j + 2], outs[2 * j + 3], both)
            other = swap(to_pair, PAIR)
            part = lax.psum_scatter(both.reshape(2, rows, n_cols), 'tp', scatter_dimension=1, tiled=True)
            moved = swap(part[1], PAIR)
            single = lax.psum_scatter((own.astype(f32) + other.astype(f32)).astype(jnp.bfloat16), 'tp',
                                      scatter_dimension=0, tiled=True)
            y_a = part[0].astype(f32) + moved.astype(f32)
            y_b = single.astype(f32)
            swapped = odd if j == 0 else 1 - odd
            y_slab = jnp.where(swapped == 0, jnp.concatenate([y_a, y_b], axis=1), jnp.concatenate([y_b, y_a], axis=1))
            col = (((chip ^ (OWNERS[j] // 2)) // 2) * (2 * n_cols)).astype(jnp.int32)
            slab = (lax.dynamic_slice_in_dim(h_last, col, 2 * n_cols, 1).astype(f32) + y_slab).astype(jnp.bfloat16)
            slab, h_last = lax.optimization_barrier((slab, h_last))
            full = lax.all_gather(slab, 'tp', axis=0, tiled=True)
            out = lax.dynamic_update_slice_in_dim(out, full, col, 1)
        return (out.reshape(n_seq, seq_len, width), k_rot.reshape(n_seq, seq_len, head_dim),
                v_val.reshape(n_seq, seq_len, head_dim))

    return jax.shard_map(
        local_layer,
        mesh=mesh,
        in_specs=(batch_spec, P(None), P('dp', 'tp'), P('dp', None), P('dp', 'tp'), P('dp', 'tp'), P('tp', 'dp'), P('tp', 'dp'), P(('part', 'dp'))),
        out_specs=(batch_spec, batch_spec, batch_spec),
        check_vma=False,
    )
```

time: 1150 us -> 1070 us (0.930)
  Pallas kernels: 0 us -> 345 us
  matrix products: 260 us -> 0 us
  waiting for transfers between devices: 753 us -> 595 us
  other arithmetic: 95.3 us -> 32.9 us
  starting transfers between devices: 0.19 us -> 45.5 us
    ppermute x0 -> x48, waiting for transfers between devices: none -> 477 us  [swap(): return lax.ppermute(x, 'dp', [(i, i ^ mask) for i in range(n_dp)])]
    all_gather x2 -> x3, waiting for transfers between devices: 543 us -> 107 us  [the longest x2 107 us: local_layer(): full = lax.all_gather(slab, 'tp', axis=0, tiled=True)]
    pallas_call x0 -> x12, Pallas kernels: none -> 345 us  [the longest x4 156 us: ffn_chunk(): pl.pallas_call(functools.partial(ffn_kernel, steps), grid=(2 * steps,), i...]
    dot_general x4 -> x0, matrix products: 260 us -> none  [the longest x1 156 us: local_layer(): jnp.einsum('bld,de->ble', normed, w_in_full, preferred_element_type=jnp.f...]
    psum x1 -> x0, waiting for transfers between devices: 210 us -> none  [local_layer(): y_sum = lax.psum(y_part, 'tp')]
    ppermute x0 -> x48, starting transfers between devices: none -> 44.6 us  [swap(): return lax.ppermute(x, 'dp', [(i, i ^ mask) for i in range(n_dp)])]
    convert_element_type x3 -> x6, other arithmetic: 34.3 us -> 12.9 us  [the longest x2 5.41 us: local_layer(): (lax.dynamic_slice_in_dim(h_last, col, 2 * n_cols, 1).astype(f32) + y_sla...]
    sub x1 -> x0, other arithmetic: 18.3 us -> none  [attend_and_gate(): jax.nn.softmax(jnp.where(key_mask, scores, MASK_VALUE), axis=-1)]
  transfers between devices with their start and end apart: 3 -> 55, of which waited for: 3 -> 17; matrix products, arithmetic and copies ran while one was open for 23% -> 5% of each run, Pallas kernels for 0% -> 29%
where the time goes in v1:
time: 1070 us
  waiting for transfers between devices  595 us (56%)
  Pallas kernels  345 us (32%)
  starting transfers between devices  45.5 us (4%)
  local copies, waits for them, and re-layouts  36.4 us (3%)
  other arithmetic  32.9 us (3%)
  between operations  14.9 us (1%)
    ppermute x48, waiting for transfers between devices, swap(): return lax.ppermute(x, 'dp', [(i, i ^ mask) for i in range(n_dp)])  477 us
    pallas_call x4, Pallas kernels, ffn_chunk(): pl.pallas_call(functools.partial(ffn_kernel, steps), grid=(2 * steps,), i...  156 us
    pallas_call x4, Pallas kernels, down_block(): pl.pallas_call(functools.partial(down_kernel, steps, joint), grid=(2 * st...  114 us
    all_gather x2, waiting for transfers between devices, local_layer(): full = lax.all_gather(slab, 'tp', axis=0, tiled=True)  107 us
    pallas_call x2, Pallas kernels, qkv_attend(): pl.pallas_call(functools.partial(qkv_kernel, head_dim, seq_len), grid=(ro...  53.5 us
    ppermute x48, starting transfers between devices, swap(): return lax.ppermute(x, 'dp', [(i, i ^ mask) for i in range(n_dp)])  44.6 us
    pallas_call x2, Pallas kernels, layer_norm(): pl.pallas_call(ln_kernel, grid=(rows // tile,), in_specs=[pl.BlockSpec((t...  21.8 us
  transfers between devices with their start and end apart: 55, of which 17 were waited for; matrix products, arithmetic and copies ran while one was open for 5% of the time, Pallas kernels for 29%

profile of v1, /device:TPU:97, one launch (start us, length us, event | category | flops | bytes accessed | tf_op | source)
XLA Modules:
  0.0 1070.4 jit_solution(1524158219713998879)
XLA Ops:
  10.9 5.4 norm.3
  18.4 63.0 %collective-permute-done = bf16[288,5120]{1,0:T(8,128)(2,1)S(1)} collective-permute-done((bf16[288,5120]{1,0:T(8,128)(2,1)}, bf16[288,5120]{1,0:T(8,128)(2,1)S(1)}, u32[]{:S(2)}, u32[]{:S(2)}) %collective-permute-start) | collective-permute-done | bytes 2949152 | tf_op jit(solution)/shard_map/ppermute | solution.py:228
  88.2 3.6 collective-permute-start.33
  95.0 7.4 constant_dynamic-slice_fusion.6
  107.6 13.1 %collective-permute-done.29.len_ref = s32[3]{0:T(128)S(1)} collective-permute-done((s32[3]{0:T(128)S(1)}, s32[3]{0:T(128)S(1)}, u32[]{:S(2)}, u32[]{:S(2)}) %collective-permute-start.29) | collective-permute-done | bytes 44 | tf_op jit(solution)/shard_map/ppermute | solution.py:228
  128.4 30.8 %collective-permute-done.23.refs_2_ = bf16[640,1280]{1,0:T(8,128)(2,1)S(1)} collective-permute-done((bf16[640,1280]{1,0:T(8,128)(2,1)}, bf16[640,1280]{1,0:T(8,128)(2,1)S(1)}, u32[]{:S(2)}, u32[]{:S(2)}) %collective-permute-start.23) | collective-permute-done | bytes 1638432 | tf_op jit(solution)/shard_map/ppermute | solution.py:228
  162.3 32.0 %collective-permute-done.16.refs_2_ = bf16[640,1280]{1,0:T(8,128)(2,1)} collective-permute-done((bf16[640,1280]{1,0:T(8,128)(2,1)}, bf16[640,1280]{1,0:T(8,128)(2,1)}, u32[]{:S(2)}, u32[]{:S(2)}) %collective-permute-start.16) | collective-permute-done | bytes 1638432 | tf_op jit(solution)/shard_map/ppermute | solution.py:228
  199.1 16.4 %norm.2.u_ref.u0 = bf16[1152,5120]{1,0:T(8,128)(2,1)} custom-call(bf16[1152,5120]{1,0:T(8,128)(2,1)} %bitcast.24, f32[1,5120]{1,0:T(1,128)} %bitcast.32), custom_call_target="tpu_custom_call" | custom-call | flops 47185920 | bytes 23592960 | tf_op jit(solution)/shard_map/norm/pallas_call | solution.py:36
  222.2 26.6 %qkv.2 = (bf16[2304,3200]{1,0:T(8,128)(2,1)}, bf16[1152,128]{1,0:T(8,128)(2,1)}, bf16[1152,128]{1,0:T(8,128)(2,1)}) custom-call(s32[1]{0:T(128)} %bitcast.2.dp_ref, s32[3]{0:T(128)} %len_ref.1, bf16[1152,5120]{1,0:T(8,128)(2,1)} %norm.2.u_ref.u0, f32[384,128]{1,0:T(8,128)} %get-tuple-element.92.cos_ref, f32[384,128]{1,0:T(8,128)} %get-tuple-element.93.sin_ref, ...), custom_call_target="tpu_custom_call" | custom-call | flops 21139292160 | bytes 20971520 | tf_op jit(solution)/shard_map/qkv/pallas_call | solution.py:101
  248.9 6.4 collective-permute-done.9.refs_2_
  260.0 30.3 %collective-permute-done.2.refs_2_ = bf16[640,1280]{1,0:T(8,128)(2,1)} collective-permute-done((bf16[640,1280]{1,0:T(8,128)(2,1)}, bf16[640,1280]{1,0:T(8,128)(2,1)}, u32[]{:S(2)}, u32[]{:S(2)}) %collective-permute-start.2) | collective-permute-done | bytes 1638432 | tf_op jit(solution)/shard_map/ppermute | solution.py:228
  294.5 26.8 %qkv.3 = (bf16[2304,3200]{1,0:T(8,128)(2,1)}, bf16[1152,128]{1,0:T(8,128)(2,1)}, bf16[1152,128]{1,0:T(8,128)(2,1)}) custom-call(s32[1]{0:T(128)} %bitcast.2.dp_ref, s32[3]{0:T(128)} %copy-done.17, bf16[1152,5120]{1,0:T(8,128)(2,1)} %all-gather.4.cloned.1.call-done.u_ref.u1, f32[384,128]{1,0:T(8,128)} %get-tuple-element.92.cos_ref, ...), custom_call_target="tpu_custom_call", output_to_operand_aliasing={{0}: (13, {})} | custom-call | flops 21139292160 | bytes 20971520 | tf_op jit(solution)/shard_map/qkv/pallas_call | solution.py:101
  321.3 4.2 collective-permute-done.4.refs_4_
  328.4 32.4 %collective-permute-done.20.refs_6_ = bf16[640,1280]{1,0:T(8,128)(2,1)} collective-permute-done((bf16[640,1280]{1,0:T(8,128)(2,1)}, bf16[640,1280]{1,0:T(8,128)(2,1)}, u32[]{:S(2)}, u32[]{:S(2)}) %collective-permute-start.20) | collective-permute-done | bytes 1638432 | tf_op jit(solution)/shard_map/ppermute | solution.py:228
  362.4 38.8 %ffn.4.refs_8_ = bf16[2304,3200]{1,0:T(8,128)(2,1)} custom-call(s32[1]{0:T(128)} %bitcast.2.dp_ref, bf16[1152,5120]{1,0:T(8,128)(2,1)} %norm.2.u_ref.u0, bf16[1152,5120]{1,0:T(8,128)(2,1)} %all-gather.4.cloned.1.call-done.u_ref.u1, bf16[640,1280]{1,0:T(8,128)(2,1)} %pad_maximum_fusion.8.refs_0_, ...), custom_call_target="tpu_custom_call", output_to_operand_aliasing={{}: (11, {})} | custom-call | flops 30198988800 | bytes 36700160 | tf_op jit(solution)/shard_map/ffn/pallas_call | solution.py:156
  405.1 39.3 %ffn.5.refs_8_ = bf16[2304,3200]{1,0:T(8,128)(2,1)} custom-call(s32[1]{0:T(128)} %bitcast.2.dp_ref, bf16[1152,5120]{1,0:T(8,128)(2,1)} %norm.2.u_ref.u0, bf16[1152,5120]{1,0:T(8,128)(2,1)} %all-gather.4.cloned.1.call-done.u_ref.u1, bf16[640,1280]{1,0:T(8,128)(2,1)} %pad_maximum_fusion.6.refs_0_, ...), custom_call_target="tpu_custom_call", output_to_operand_aliasing={{}: (11, {})} | custom-call | flops 30198988800 | bytes 36700160 | tf_op jit(solution)/shard_map/ffn/pallas_call | solution.py:156
  445.6 38.8 %ffn.6.refs_8_ = bf16[2304,3200]{1,0:T(8,128)(2,1)} custom-call(s32[1]{0:T(128)} %bitcast.2.dp_ref, bf16[1152,5120]{1,0:T(8,128)(2,1)} %norm.2.u_ref.u0, bf16[1152,5120]{1,0:T(8,128)(2,1)} %all-gather.4.cloned.1.call-done.u_ref.u1, bf16[640,1280]{1,0:T(8,128)(2,1)} %pad_maximum_fusion.4.refs_0_, ...), custom_call_target="tpu_custom_call", output_to_operand_aliasing={{}: (11, {})} | custom-call | flops 30198988800 | bytes 36700160 | tf_op jit(solution)/shard_map/ffn/pallas_call | solution.py:156
  484.4 7.3 collective-permute-done.37.w0
  492.6 39.1 %ffn.7.x_ref = bf16[2304,3200]{1,0:T(8,128)(2,1)} custom-call(s32[1]{0:T(128)} %bitcast.2.dp_ref, bf16[1152,5120]{1,0:T(8,128)(2,1)} %norm.2.u_ref.u0, bf16[1152,5120]{1,0:T(8,128)(2,1)} %all-gather.4.cloned.1.call-done.u_ref.u1, bf16[640,1280]{1,0:T(8,128)(2,1)} %pad_maximum_fusion.2.refs_0_, ...), custom_call_target="tpu_custom_call", output_to_operand_aliasing={{}: (11, {})} | custom-call | flops 30198988800 | bytes 36700160 | tf_op jit(solution)/shard_map/ffn/pallas_call | solution.py:156
  531.7 28.5 %down.4 = (bf16[2304,1280]{1,0:T(8,128)(2,1)}, bf16[1152,1280]{1,0:T(8,128)(2,1)}) custom-call(s32[1]{0:T(128)} %bitcast.1.core_ref, bf16[2304,3200]{1,0:T(8,128)(2,1)} %ffn.7.x_ref, bf16[3200,640]{1,0:T(8,128)(2,1)} %pad_maximum_fusion.w0, bf16[3200,640]{1,0:T(8,128)(2,1)} %collective-permute-done.39.w1), custom_call_target="tpu_custom_call" | custom-call | flops 18874368000 | bytes 28835840 | tf_op jit(solution)/shard_map/down/pallas_call | solution.py:207
  560.3 28.5 %down.5 = (bf16[2304,1280]{1,0:T(8,128)(2,1)}, bf16[1152,1280]{1,0:T(8,128)(2,1)}) custom-call(s32[1]{0:T(128)} %bitcast.1.core_ref, bf16[2304,3200]{1,0:T(8,128)(2,1)} %ffn.7.x_ref, bf16[3200,640]{1,0:T(8,128)(2,1)} %collective-permute-done.37.w0, bf16[3200,640]{1,0:T(8,128)(2,1)} %collective-permute-done.38.w1, ...), custom_call_target="tpu_custom_call", output_to_operand_aliasing={{0}: (4, {})} | custom-call | flops 18874368000 | bytes 28835840 | tf_op jit(solution)/shard_map/down/pallas_call | solution.py:207
  592.1 88.6 %collective-permute-done.44.w0 = bf16[3200,640]{1,0:T(8,128)(2,1)} collective-permute-done((bf16[3200,640]{1,0:T(8,128)(2,1)}, bf16[3200,640]{1,0:T(8,128)(2,1)}, u32[]{:S(2)}, u32[]{:S(2)}) %collective-permute-start.44) | collective-permute-done | bytes 4096032 | tf_op jit(solution)/shard_map/ppermute | solution.py:228
  684.8 83.8 %collective-permute-done.42.w0 = bf16[3200,640]{1,0:T(8,128)(2,1)} collective-permute-done((bf16[3200,640]{1,0:T(8,128)(2,1)}, bf16[3200,640]{1,0:T(8,128)(2,1)}, u32[]{:S(2)}, u32[]{:S(2)}) %collective-permute-start.42) | collective-permute-done | bytes 4096032 | tf_op jit(solution)/shard_map/ppermute | solution.py:228
  769.4 28.6 %down.6 = (bf16[2304,1280]{1,0:T(8,128)(2,1)}, bf16[1152,1280]{1,0:T(8,128)(2,1)}) custom-call(s32[1]{0:T(128)} %bitcast.1.core_ref, bf16[2304,3200]{1,0:T(8,128)(2,1)} %ffn.7.x_ref, bf16[3200,640]{1,0:T(8,128)(2,1)} %collective-permute-done.44.w0, bf16[3200,640]{1,0:T(8,128)(2,1)} %collective-permute-done.45.w1), custom_call_target="tpu_custom_call" | custom-call | flops 18874368000 | bytes 28835840 | tf_op jit(solution)/shard_map/down/pallas_call | solution.py:207
  799.9 28.5 %down.7 = (bf16[2304,1280]{1,0:T(8,128)(2,1)}, bf16[1152,1280]{1,0:T(8,128)(2,1)}) custom-call(s32[1]{0:T(128)} %bitcast.1.core_ref, bf16[2304,3200]{1,0:T(8,128)(2,1)} %ffn.7.x_ref, bf16[3200,640]{1,0:T(8,128)(2,1)} %collective-permute-done.42.w0, bf16[3200,640]{1,0:T(8,128)(2,1)} %copy-done.12, ...), custom_call_target="tpu_custom_call", output_to_operand_aliasing={{0}: (4, {})} | custom-call | flops 18874368000 | bytes 28835840 | tf_op jit(solution)/shard_map/down/pallas_call | solution.py:207
  828.7 65.6 %collective-permute-done.47 = bf16[1152,1280]{1,0:T(8,128)(2,1)S(1)} collective-permute-done((bf16[1152,1280]{1,0:T(8,128)(2,1)}, bf16[1152,1280]{1,0:T(8,128)(2,1)S(1)}, u32[]{:S(2)}, u32[]{:S(2)}) %collective-permute-start.47) | collective-permute-done | bytes 2949152 | tf_op jit(solution)/shard_map/ppermute | solution.py:228
  899.9 15.8 %collective-permute-done.40 = bf16[288,1280]{1,0:T(8,128)(2,1)S(1)} collective-permute-done((bf16[288,1280]{1,0:T(8,128)(2,1)S(1)}, bf16[288,1280]{1,0:T(8,128)(2,1)S(1)}, u32[]{:S(2)}, u32[]{:S(2)}) %collective-permute-start.40) | collective-permute-done | bytes 737312 | tf_op jit(solution)/shard_map/ppermute | solution.py:228
  922.4 11.7 %reduce-scatter.11.cloned.1.call-done = bf16[288,1280]{1,0:T(8,128)(2,1)} async-done(((bf16[1152,1280]{1,0:T(8,128)(2,1)}), bf16[288,1280]{1,0:T(8,128)(2,1)}) %reduce-scatter.11.cloned.1.call-update) | async-done | bytes 737296 | tf_op jit(solution)/shard_map/reduce_scatter | solution.py:301
  942.0 53.6 %all-gather.6.cloned.1.call-done = bf16[1152,2560]{1,0:T(8,128)(2,1)} async-done(((bf16[288,2560]{1,0:T(8,128)(2,1)}), bf16[1152,2560]{1,0:T(8,128)(2,1)}) %all-gather.6.cloned.1.call-update) | async-done | bytes 5898256 | tf_op jit(solution)/shard_map/all_gather | solution.py:310
  995.6 6.0 broadcast_in_dim.2
  1004.6 53.1 %all-gather.8.cloned.1.call-done = bf16[1152,2560]{1,0:T(8,128)(2,1)} async-done(((bf16[288,2560]{1,0:T(8,128)(2,1)}), bf16[1152,2560]{1,0:T(8,128)(2,1)}) %all-gather.8.cloned.1.call-update) | async-done | bytes 5898256 | tf_op jit(solution)/shard_map/all_gather | solution.py:310
  1057.6 5.6 constant_dynamic-update-slice_fusion
  (169 shorter events, 96.0 us)
Async XLA Ops:
  7.2 287.3 %all-gather.4.cloned.1.call-start = ((), (), s32[]{:S(2)}) async-start(), calls=%async_computation.4 | async-start | bytes 14745600 | tf_op jit(solution)/shard_map/all_gather | solution.py:272
  16.3 65.1 %collective-permute-start = (bf16[288,5120]{1,0:T(8,128)(2,1)}, bf16[288,5120]{1,0:T(8,128)(2,1)S(1)}, u32[]{:S(2)}, u32[]{:S(2)}) collective-permute-start(bf16[288,5120]{1,0:T(8,128)(2,1)} %norm.3), channel_id=1, source_target_pairs={{0,2},{1,3},{2,0},{3,1},{4,6},{5,7},{6,4},{7,5},{8,10},{9,11},{10,... | collective-permute-start | bytes 8847368 | tf_op jit(solution)/shard_map/ppermute | solution.py:228
  83.0 813.9 %reduce-scatter.5.cloned.1.call-start = ((), (), s32[]{:S(2)}) async-start(), calls=%async_computation.5 | async-start | bytes 7372800 | tf_op jit(solution)/shard_map/reduce_scatter | solution.py:299
  105.0 54.2 %collective-permute-start.25 = (bf16[640,1280]{1,0:T(8,128)(2,1)}, bf16[640,1280]{1,0:T(8,128)(2,1)}, u32[]{:S(2)}, u32[]{:S(2)}) collective-permute-start(bf16[640,1280]{1,0:T(8,128)(2,1)} %pad_maximum_fusion.8.refs_0_), channel_id=1, source_target_pairs={{0,6},{1,7},{2,4},{3,5},{4,2},{5,3},{6,0},{7,1},{8,14},{9,15},{10,... | collective-permute-start | bytes 4915208 | tf_op jit(solution)/shard_map/ppermute | solution.py:228
  121.6 72.7 %collective-permute-start.16 = (bf16[640,1280]{1,0:T(8,128)(2,1)}, bf16[640,1280]{1,0:T(8,128)(2,1)}, u32[]{:S(2)}, u32[]{:S(2)}) collective-permute-start(bf16[640,1280]{1,0:T(8,128)(2,1)} %pad_maximum_fusion.7), channel_id=1, source_target_pairs={{0,2},{1,3},{2,0},{3,1},{4,6},{5,7},{6,4},{7,5},{8,10},{9,11},{10,... | collective-permute-start | bytes 4915208 | tf_op jit(solution)/shard_map/ppermute | solution.py:228
  123.6 71.6 %collective-permute-start.35 = (bf16[640,896]{1,0:T(8,128)(2,1)}, bf16[640,896]{1,0:T(8,128)(2,1)}, u32[]{:S(2)}, u32[]{:S(2)}) collective-permute-start(bf16[640,896]{1,0:T(8,128)(2,1)} %collective-permute-done.31.refs_2_), channel_id=1, source_target_pairs={{0,6},{1,7},{2,4},{3,5},{4,2},{5,3},{6,0},{7,1},{8,14},{9,15},{10,... | collective-permute-start | bytes 3440648 | tf_op jit(solution)/shard_map/ppermute | solution.py:228
  159.1 58.1 %collective-permute-start.18 = (bf16[640,1280]{1,0:T(8,128)(2,1)}, bf16[640,1280]{1,0:T(8,128)(2,1)}, u32[]{:S(2)}, u32[]{:S(2)}) collective-permute-start(bf16[640,1280]{1,0:T(8,128)(2,1)} %pad_maximum_fusion.6.refs_0_), channel_id=1, source_target_pairs={{0,6},{1,7},{2,4},{3,5},{4,2},{5,3},{6,0},{7,1},{8,14},{9,15},{10,... | collective-permute-start | bytes 4915208 | tf_op jit(solution)/shard_map/ppermute | solution.py:228
  159.1 58.2 %collective-permute-start.15 = (bf16[640,1280]{1,0:T(8,128)(2,1)}, bf16[640,1280]{1,0:T(8,128)(2,1)}, u32[]{:S(2)}, u32[]{:S(2)}) collective-permute-start(bf16[640,1280]{1,0:T(8,128)(2,1)} %pad_maximum_fusion.6.refs_0_), channel_id=1, source_target_pairs={{0,1},{1,0},{2,3},{3,2},{4,5},{5,4},{6,7},{7,6},{8,9},{9,8},{10,11... | collective-permute-start | bytes 4915208 | tf_op jit(solution)/shard_map/ppermute | solution.py:228
  162.0 55.9 %collective-permute-start.32 = (bf16[640,896]{1,0:T(8,128)(2,1)}, bf16[640,896]{1,0:T(8,128)(2,1)}, u32[]{:S(2)}, u32[]{:S(2)}) collective-permute-start(bf16[640,896]{1,0:T(8,128)(2,1)} %collective-permute-done.31.refs_2_), channel_id=1, source_target_pairs={{0,1},{1,0},{2,3},{3,2},{4,5},{5,4},{6,7},{7,6},{8,9},{9,8},{10,11... | collective-permute-start | bytes 3440648 | tf_op jit(solution)/shard_map/ppermute | solution.py:228
  218.0 72.3 %collective-permute-start.2 = (bf16[640,1280]{1,0:T(8,128)(2,1)}, bf16[640,1280]{1,0:T(8,128)(2,1)}, u32[]{:S(2)}, u32[]{:S(2)}) collective-permute-start(bf16[640,1280]{1,0:T(8,128)(2,1)} %pad_maximum_fusion.3), channel_id=1, source_target_pairs={{0,2},{1,3},{2,0},{3,1},{4,6},{5,7},{6,4},{7,5},{8,10},{9,11},{10,... | collective-permute-start | bytes 4915208 | tf_op jit(solution)/shard_map/ppermute | solution.py:228
  219.4 73.8 %collective-permute-start.27 = (bf16[640,1280]{1,0:T(8,128)(2,1)}, bf16[640,1280]{1,0:T(8,128)(2,1)}, u32[]{:S(2)}, u32[]{:S(2)}) collective-permute-start(bf16[640,1280]{1,0:T(8,128)(2,1)} %copy-done.13), channel_id=1, source_target_pairs={{0,6},{1,7},{2,4},{3,5},{4,2},{5,3},{6,0},{7,1},{8,14},{9,15},{10,... | collective-permute-start | bytes 4915208 | tf_op jit(solution)/shard_map/ppermute | solution.py:228
  255.2 70.3 %collective-permute-start.4 = (bf16[640,1280]{1,0:T(8,128)(2,1)}, bf16[640,1280]{1,0:T(8,128)(2,1)S(1)}, u32[]{:S(2)}, u32[]{:S(2)}) collective-permute-start(bf16[640,1280]{1,0:T(8,128)(2,1)} %pad_maximum_fusion.2.refs_0_), channel_id=1, source_target_pairs={{0,6},{1,7},{2,4},{3,5},{4,2},{5,3},{6,0},{7,1},{8,14},{9,15},{10,... | collective-permute-start | bytes 4915208 | tf_op jit(solution)/shard_map/ppermute | solution.py:228
  258.1 69.8 %collective-permute-start.24 = (bf16[640,1280]{1,0:T(8,128)(2,1)}, bf16[640,1280]{1,0:T(8,128)(2,1)}, u32[]{:S(2)}, u32[]{:S(2)}) collective-permute-start(bf16[640,1280]{1,0:T(8,128)(2,1)} %copy-done.13), channel_id=1, source_target_pairs={{0,1},{1,0},{2,3},{3,2},{4,5},{5,4},{6,7},{7,6},{8,9},{9,8},{10,11... | collective-permute-start | bytes 4915208 | tf_op jit(solution)/shard_map/ppermute | solution.py:228
  259.9 68.1 %collective-permute-start.26 = (bf16[640,1280]{1,0:T(8,128)(2,1)}, bf16[640,1280]{1,0:T(8,128)(2,1)S(1)}, u32[]{:S(2)}, u32[]{:S(2)}) collective-permute-start(bf16[640,1280]{1,0:T(8,128)(2,1)} %collective-permute-done.25.refs_4_), channel_id=1, source_target_pairs={{0,1},{1,0},{2,3},{3,2},{4,5},{5,4},{6,7},{7,6},{8,9},{9,8},{10,11... | collective-permute-start | bytes 4915208 | tf_op jit(solution)/shard_map/ppermute | solution.py:228
  290.3 70.4 %collective-permute-start.20 = (bf16[640,1280]{1,0:T(8,128)(2,1)}, bf16[640,1280]{1,0:T(8,128)(2,1)}, u32[]{:S(2)}, u32[]{:S(2)}) collective-permute-start(bf16[640,1280]{1,0:T(8,128)(2,1)} %collective-permute-done.16.refs_2_), channel_id=1, source_target_pairs={{0,6},{1,7},{2,4},{3,5},{4,2},{5,3},{6,0},{7,1},{8,14},{9,15},{10,... | collective-permute-start | bytes 4915208 | tf_op jit(solution)/shard_map/ppermute | solution.py:228
  293.2 67.9 %collective-permute-start.28 = (bf16[640,1280]{1,0:T(8,128)(2,1)}, bf16[640,1280]{1,0:T(8,128)(2,1)}, u32[]{:S(2)}, u32[]{:S(2)}) collective-permute-start(bf16[640,1280]{1,0:T(8,128)(2,1)} %collective-permute-done.27.refs_6_), channel_id=1, source_target_pairs={{0,1},{1,0},{2,3},{3,2},{4,5},{5,4},{6,7},{7,6},{8,9},{9,8},{10,11... | collective-permute-start | bytes 4915208 | tf_op jit(solution)/shard_map/ppermute | solution.py:228
  325.6 75.7 %collective-permute-start.1 = (bf16[640,1280]{1,0:T(8,128)(2,1)}, bf16[640,1280]{1,0:T(8,128)(2,1)}, u32[]{:S(2)}, u32[]{:S(2)}) collective-permute-start(bf16[640,1280]{1,0:T(8,128)(2,1)} %pad_maximum_fusion.2.refs_0_), channel_id=1, source_target_pairs={{0,1},{1,0},{2,3},{3,2},{4,5},{5,4},{6,7},{7,6},{8,9},{9,8},{10,11... | collective-permute-start | bytes 4915208 | tf_op jit(solution)/shard_map/ppermute | solution.py:228
  327.9 73.5 %collective-permute-start.17 = (bf16[640,1280]{1,0:T(8,128)(2,1)}, bf16[640,1280]{1,0:T(8,128)(2,1)}, u32[]{:S(2)}, u32[]{:S(2)}) collective-permute-start(bf16[640,1280]{1,0:T(8,128)(2,1)} %collective-permute-done.16.refs_2_), channel_id=1, source_target_pairs={{0,1},{1,0},{2,3},{3,2},{4,5},{5,4},{6,7},{7,6},{8,9},{9,8},{10,11... | collective-permute-start | bytes 4915208 | tf_op jit(solution)/shard_map/ppermute | solution.py:228
  328.0 73.6 %collective-permute-start.19 = (bf16[640,1280]{1,0:T(8,128)(2,1)}, bf16[640,1280]{1,0:T(8,128)(2,1)}, u32[]{:S(2)}, u32[]{:S(2)}) collective-permute-start(bf16[640,1280]{1,0:T(8,128)(2,1)} %collective-permute-done.18.refs_4_), channel_id=1, source_target_pairs={{0,1},{1,0},{2,3},{3,2},{4,5},{5,4},{6,7},{7,6},{8,9},{9,8},{10,11... | collective-permute-start | bytes 4915208 | tf_op jit(solution)/shard_map/ppermute | solution.py:228
  401.3 90.4 %collective-permute-start.37 = (bf16[3200,640]{1,0:T(8,128)(2,1)}, bf16[3200,640]{1,0:T(8,128)(2,1)}, u32[]{:S(2)}, u32[]{:S(2)}) collective-permute-start(bf16[3200,640]{1,0:T(8,128)(2,1)} %pad_maximum_fusion.1), channel_id=1, source_target_pairs={{0,2},{1,3},{2,0},{3,1},{4,6},{5,7},{6,4},{7,5},{8,10},{9,11},{10,... | collective-permute-start | bytes 12288008 | tf_op jit(solution)/shard_map/ppermute | solution.py:228
  444.4 87.3 %collective-permute-start.39 = (bf16[3200,640]{1,0:T(8,128)(2,1)S(1)}, bf16[3200,640]{1,0:T(8,128)(2,1)}, u32[]{:S(2)}, u32[]{:S(2)}) collective-permute-start(bf16[3200,640]{1,0:T(8,128)(2,1)S(1)} %copy-done.2), channel_id=1, source_target_pairs={{0,1},{1,0},{2,3},{3,2},{4,5},{5,4},{6,7},{7,6},{8,9},{9,8},{10,11... | collective-permute-start | bytes 12288008 | tf_op jit(solution)/shard_map/ppermute | solution.py:228
  491.6 68.6 %collective-permute-start.38 = (bf16[3200,640]{1,0:T(8,128)(2,1)}, bf16[3200,640]{1,0:T(8,128)(2,1)}, u32[]{:S(2)}, u32[]{:S(2)}) collective-permute-start(bf16[3200,640]{1,0:T(8,128)(2,1)} %collective-permute-done.37.w0), channel_id=1, source_target_pairs={{0,1},{1,0},{2,3},{3,2},{4,5},{5,4},{6,7},{7,6},{8,9},{9,8},{10,11... | collective-permute-start | bytes 12288008 | tf_op jit(solution)/shard_map/ppermute | solution.py:228
  588.8 309.8 %reduce-scatter.7.cloned.1.call-start = ((), (), s32[]{:S(2)}) async-start(), calls=%async_computation.6 | async-start | bytes 3686400 | tf_op jit(solution)/shard_map/reduce_scatter | solution.py:301
  589.1 91.7 %collective-permute-start.44 = (bf16[3200,640]{1,0:T(8,128)(2,1)}, bf16[3200,640]{1,0:T(8,128)(2,1)}, u32[]{:S(2)}, u32[]{:S(2)}) collective-permute-start(bf16[3200,640]{1,0:T(8,128)(2,1)} %pad_maximum_fusion.w0), channel_id=1, source_target_pairs={{0,6},{1,7},{2,4},{3,5},{4,2},{5,3},{6,0},{7,1},{8,14},{9,15},{10,... | collective-permute-start | bytes 12288008 | tf_op jit(solution)/shard_map/ppermute | solution.py:228
  591.9 90.2 %collective-permute-start.41 = (bf16[1152,1280]{1,0:T(8,128)(2,1)}, bf16[1152,1280]{1,0:T(8,128)(2,1)S(1)}, u32[]{:S(2)}, u32[]{:S(2)}) collective-permute-start(bf16[1152,1280]{1,0:T(8,128)(2,1)} %get-tuple-element.47), channel_id=1, source_target_pairs={{0,2},{1,3},{2,0},{3,1},{4,6},{5,7},{6,4},{7,5},{8,10},{9,11},{10,... | collective-permute-start | bytes 8847368 | tf_op jit(solution)/shard_map/ppermute | solution.py:228
  591.9 176.7 %collective-permute-start.42 = (bf16[3200,640]{1,0:T(8,128)(2,1)}, bf16[3200,640]{1,0:T(8,128)(2,1)}, u32[]{:S(2)}, u32[]{:S(2)}) collective-permute-start(bf16[3200,640]{1,0:T(8,128)(2,1)} %collective-permute-done.37.w0), channel_id=1, source_target_pairs={{0,6},{1,7},{2,4},{3,5},{4,2},{5,3},{6,0},{7,1},{8,14},{9,15},{10,... | collective-permute-start | bytes 12288008 | tf_op jit(solution)/shard_map/ppermute | solution.py:228
  680.8 88.6 %collective-permute-start.45 = (bf16[3200,640]{1,0:T(8,128)(2,1)}, bf16[3200,640]{1,0:T(8,128)(2,1)}, u32[]{:S(2)}, u32[]{:S(2)}) collective-permute-start(bf16[3200,640]{1,0:T(8,128)(2,1)} %collective-permute-done.44.w0), channel_id=1, source_target_pairs={{0,1},{1,0},{2,3},{3,2},{4,5},{5,4},{6,7},{7,6},{8,9},{9,8},{10,11... | collective-permute-start | bytes 12288008 | tf_op jit(solution)/shard_map/ppermute | solution.py:228
  684.7 235.1 %reduce-scatter.9.cloned.1.call-start = ((), (), s32[]{:S(2)}) async-start(), calls=%async_computation.8 | async-start | bytes 7372800 | tf_op jit(solution)/shard_map/reduce_scatter | solution.py:299
  828.5 105.7 %reduce-scatter.11.cloned.1.call-start = ((), (), s32[]{:S(2)}) async-start(), calls=%async_computation.9 | async-start | bytes 3686400 | tf_op jit(solution)/shard_map/reduce_scatter | solution.py:301
  828.5 65.7 %collective-permute-start.47 = (bf16[1152,1280]{1,0:T(8,128)(2,1)}, bf16[1152,1280]{1,0:T(8,128)(2,1)S(1)}, u32[]{:S(2)}, u32[]{:S(2)}) collective-permute-start(bf16[1152,1280]{1,0:T(8,128)(2,1)} %get-tuple-element.53), channel_id=1, source_target_pairs={{0,2},{1,3},{2,0},{3,1},{4,6},{5,7},{6,4},{7,5},{8,10},{9,11},{10,... | collective-permute-start | bytes 8847368 | tf_op jit(solution)/shard_map/ppermute | solution.py:228
  896.9 98.8 %all-gather.6.cloned.1.call-start = ((), (), s32[]{:S(2)}) async-start(), calls=%async_computation.7 | async-start | bytes 7372800 | tf_op jit(solution)/shard_map/all_gather | solution.py:310
  919.5 138.2 %all-gather.8.cloned.1.call-start = ((), (), s32[]{:S(2)}) async-start(), calls=%async_computation.10 | async-start | bytes 7372800 | tf_op jit(solution)/shard_map/all_gather | solution.py:310
  (43 other events, 1260.5 us)
Sparse Core Ops, SparseCore 0:
  83.1 113.8 all-gather.3
  589.0 60.5 reduce-scatter.4
  684.8 36.4 reduce-scatter.6
  828.6 60.5 reduce-scatter.8
  897.0 37.1 reduce-scatter.10
  936.1 59.4 all-gather.5
  997.2 60.3 all-gather.7

commit v2 on v1

--- a/solution.py
+++ b/solution.py
@@ -168,11 +168,10 @@
     )(dp, u_own, u_pair, *blocks, mixed)
 
 
-def down_kernel(steps, joint, core_ref, x_ref, w0, w1, *refs):
-    both_ref, solo_ref, wbuf, sem = refs[-4:]
-    i = pl.program_id(0)
-
-    @pl.when(i == 0)
+def down_kernel(core_ref, x_ref, w0, w1, *refs):
+    y_ref, wbuf, sem = refs[-3:]
+
+    @pl.when(pl.program_id(0) == 0)
     def _():
         n = w0.shape[1]
         copies = []
@@ -184,40 +183,62 @@
         for c in copies:
             c.wait()
 
-    y = jnp.dot(x_ref[...], wbuf[...], preferred_element_type=jnp.float32).astype(jnp.bfloat16)
-
-    @pl.when(i // steps == joint)
-    def _():
-        both_ref[...] = y
-
-    @pl.when(i // steps != joint)
-    def _():
-        solo_ref[...] = y
-
-
-def down_block(core, mixed, w0, w1, both=None):
+    y_ref[...] = jnp.dot(x_ref[...], wbuf[...], preferred_element_type=jnp.float32).astype(jnp.bfloat16)
+
+
+def down_block(core, mixed, token_set, weights, out_sets=1, out_set=0, dest=None):
     depth = mixed.shape[1]
-    n = w0.shape[1]
+    n = weights[0].shape[1]
     rows, steps = mixed.shape[0] // 2, 2
     tile = rows // steps
-    joint = 0 if both is None else 1
-    first = joint * steps
+    given = [] if dest is None else [dest]
     anywhere = pl.BlockSpec(memory_space=pl.ANY)
-    hold = lambda i, start: jnp.clip(i - start, 0, steps - 1)
-    return pl.pallas_call(
-        functools.partial(down_kernel, steps, joint),
-        grid=(2 * steps,),
-        in_specs=[pl.BlockSpec(memory_space=pltpu.SMEM), pl.BlockSpec((tile, depth), lambda i: (i, 0))]
-        + [anywhere] * (2 + joint),
-        out_specs=[pl.BlockSpec((tile, 2 * n), lambda i: (first + hold(i, first), 0)),
-                   pl.BlockSpec((tile, 2 * n), lambda i: (hold(i, steps - first), 0))],
-        out_shape=[jax.ShapeDtypeStruct((2 * rows, 2 * n), jnp.bfloat16), jax.ShapeDtypeStruct((rows, 2 * n), jnp.bfloat16)],
+    return pl.pallas_call(
+        down_kernel,
+        grid=(steps,),
+        in_specs=[pl.BlockSpec(memory_space=pltpu.SMEM), pl.BlockSpec((tile, depth), lambda i: (token_set * steps + i, 0))]
+        + [anywhere] * (2 + len(given)),
+        out_specs=pl.BlockSpec((tile, 2 * n), lambda i: (out_set * steps + i, 0)),
+        out_shape=jax.ShapeDtypeStruct((out_sets * rows, 2 * n), jnp.bfloat16),
         scratch_shapes=[pltpu.VMEM((depth, 2 * n), jnp.bfloat16), pltpu.SemaphoreType.DMA((2,))],
-        input_output_aliases={4: 0} if joint else {},
+        input_output_aliases={4: 0} if given else {},
         compiler_params=pltpu.CompilerParams(vmem_limit_bytes=VMEM_LIMIT),
-        cost_estimate=cost(8 * rows * depth * n, 4 * (rows * depth + depth * n + 2 * rows * n)),
+        cost_estimate=cost(4 * rows * depth * n, 2 * (rows * depth + 2 * depth * n + 2 * rows * n)),
         name="down",
-    )(core, mixed, w0, w1, *([] if both is None else [both]))
+    )(core, mixed, *weights, *given)
+
+
+def place_kernel(at_ref, *refs):
+    pieces, (out_ref, sem) = refs[:5], refs[-2:]
+    quarter, cols = pieces[3].shape
+    copies = []
+    for k, (mask, start) in enumerate(((0, 0), (1, 0), (3, 0), (2, 0), (2, cols))):
+        row = pl.multiple_of((at_ref[0] ^ mask) * quarter, quarter)
+        col = pl.multiple_of(at_ref[1] + start, cols)
+        copies.append(pltpu.make_async_copy(
+            pieces[k], out_ref.at[pl.ds(row, quarter), pl.ds(col, pieces[k].shape[1])], sem.at[k]))
+    for c in copies:
+        c.start()
+    for c in copies:
+        c.wait()
+
+
+def place(at, pieces, n_tp, width, out=None):
+    quarter = pieces[0].shape[0]
+    given = [] if out is None else [out]
+    anywhere = pl.BlockSpec(memory_space=pl.ANY)
+    return pl.pallas_call(
+        place_kernel,
+        in_specs=[pl.BlockSpec(memory_space=pltpu.SMEM)] + [pl.BlockSpec(memory_space=pltpu.VMEM)] * 5
+        + [anywhere] * len(given),
+        out_specs=anywhere,
+        out_shape=jax.ShapeDtypeStruct((n_tp * quarter, width), jnp.bfloat16),
+        scratch_shapes=[pltpu.SemaphoreType.DMA((5,))],
+        input_output_aliases={6: 0} if given else {},
+        compiler_params=pltpu.CompilerParams(vmem_limit_bytes=VMEM_LIMIT),
+        cost_estimate=cost(quarter * width, 4 * quarter * width),
+        name="place",
+    )(at, *pieces, *given)
 
 
 def solution(mesh):
@@ -226,6 +247,9 @@
 
     def swap(x, mask):
         return lax.ppermute(x, 'dp', [(i, i ^ mask) for i in range(n_dp)])
+
+    def swap_tp(x, mask):
+        return lax.ppermute(x, 'tp', [(i, i ^ mask) for i in range(n_tp)])
 
     def local_layer(hidden, ln_scale, w_q, w_kv, w_gate, w_up, w_o, w_down, prompt_len):
         n_seq, seq_len, width = hidden.shape
@@ -289,17 +313,20 @@
 
         f32 = jnp.float32
         n_cols = 2 * out_cols
-        out = jnp.zeros((rows, width), jnp.bfloat16)
+        out = None
         odd = chip % 2
         h_last = h_quarter
         for j in (0, 2):
-            both, to_pair = down_block(core_arr, mixed, outs[2 * j], outs[2 * j + 1])
-            both, own = down_block(core_arr, mixed, outs[2 * j + 2], outs[2 * j + 3], both)
+            first, second = outs[2 * j:2 * j + 2], outs[2 * j + 2:2 * j + 4]
+            to_pair = down_block(core_arr, mixed, 1, first)
             other = swap(to_pair, PAIR)
+            both = down_block(core_arr, mixed, 0, first, 2, 0)
+            both = down_block(core_arr, mixed, 1, second, 2, 1, both)
+            own = down_block(core_arr, mixed, 0, second)
             part = lax.psum_scatter(both.reshape(2, rows, n_cols), 'tp', scatter_dimension=1, tiled=True)
             moved = swap(part[1], PAIR)
-            single = lax.psum_scatter((own.astype(f32) + other.astype(f32)).astype(jnp.bfloat16), 'tp',
-                                      scatter_dimension=0, tiled=True)
+            joined = (own.astype(f32) + other.astype(f32)).astype(jnp.bfloat16)
+            single = lax.psum_scatter(joined, 'tp', scatter_dimension=0, tiled=True)
             y_a = part[0].astype(f32) + moved.astype(f32)
             y_b = single.astype(f32)
             swapped = odd if j == 0 else 1 - odd
@@ -307,8 +334,12 @@
             col = (((chip ^ (OWNERS[j] // 2)) // 2) * (2 * n_cols)).astype(jnp.int32)
             slab = (lax.dynamic_slice_in_dim(h_last, col, 2 * n_cols, 1).astype(f32) + y_slab).astype(jnp.bfloat16)
             slab, h_last = lax.optimization_barrier((slab, h_last))
-            full = lax.all_gather(slab, 'tp', axis=0, tiled=True)
-            out = lax.dynamic_update_slice_in_dim(out, full, col, 1)
+            from_1 = swap_tp(slab, 1)
+            from_3 = swap_tp(slab, 3)
+            far_lo = swap_tp(from_1[:, :n_cols], 3)
+            far_hi = swap_tp(from_3[:, n_cols:], 1)
+            at = jnp.stack([tp.astype(jnp.int32), col])
+            out = place(at, (slab, from_1, from_3, far_lo, far_hi), n_tp, width, out)
         return (out.reshape(n_seq, seq_len, width), k_rot.reshape(n_seq, seq_len, head_dim),
                 v_val.reshape(n_seq, seq_len, head_dim))
 

time: 1070 us -> 1120 us (1.047)
  Pallas kernels: 345 us -> 380 us
  starting transfers between devices: 45.5 us -> 64.9 us
  local copies, waits for them, and re-layouts: 36.4 us -> 21.6 us
    all_gather x2 -> x0, waiting for transfers between devices: 107 us -> none  [local_layer(): full = lax.all_gather(slab, 'tp', axis=0, tiled=True)]
    ppermute x0 -> x8, waiting for transfers between devices: none -> 73.3 us  [swap_tp(): return lax.ppermute(x, 'tp', [(i, i ^ mask) for i in range(n_tp)])]
    reduce_scatter x2, waiting for transfers between devices: 0.04 us -> 57.1 us  [local_layer(): lax.psum_scatter(both.reshape(2, rows, n_cols), 'tp', scatter_dimension=1...]
    pallas_call x4 -> x10, Pallas kernels: 114 us -> 148 us  [the longest x8 138 us: down_block(): pl.pallas_call(down_kernel, grid=(steps,), in_specs=[pl.BlockSpec(memory_...]
    ppermute x48, starting transfers between devices: 44.6 us -> 59.9 us  [swap(): return lax.ppermute(x, 'dp', [(i, i ^ mask) for i in range(n_dp)])]
    reduce_scatter x2, waiting for transfers between devices: 11.7 us -> 0.01 us  [local_layer(): single = lax.psum_scatter(joined, 'tp', scatter_dimension=0, tiled=True)]
  transfers between devices with their start and end apart: 55 -> 61, of which waited for: 17 -> 21; matrix products, arithmetic and copies ran while one was open for 5% -> 4% of each run, Pallas kernels for 29% -> 32%
where the time goes in v2:
time: 1120 us; the launch traced here: 1110 us
  waiting for transfers between devices  601 us (54%)
  Pallas kernels  380 us (34%)
  starting transfers between devices  64.9 us (6%)
  other arithmetic  31.9 us (3%)
  local copies, waits for them, and re-layouts  21.6 us (2%)
  between operations  15 us (1%)
    ppermute x48, waiting for transfers between devices, swap(): return lax.ppermute(x, 'dp', [(i, i ^ mask) for i in range(n_dp)])  471 us
    pallas_call x4, Pallas kernels, ffn_chunk(): pl.pallas_call(functools.partial(ffn_kernel, steps), grid=(2 * steps,), i...  156 us
    pallas_call x8, Pallas kernels, down_block(): pl.pallas_call(down_kernel, grid=(steps,), in_specs=[pl.BlockSpec(memory_...  138 us
    ppermute x8, waiting for transfers between devices, swap_tp(): return lax.ppermute(x, 'tp', [(i, i ^ mask) for i in range(n_tp)])  73.3 us
    ppermute x48, starting transfers between devices, swap(): return lax.ppermute(x, 'dp', [(i, i ^ mask) for i in range(n_dp)])  59.9 us
    reduce_scatter x2, waiting for transfers between devices, local_layer(): lax.psum_scatter(both.reshape(2, rows, n_cols), 'tp', scatter_dimension=1...  57.1 us
    pallas_call x2, Pallas kernels, qkv_attend(): pl.pallas_call(functools.partial(qkv_kernel, head_dim, seq_len), grid=(ro...  53.4 us
  transfers between devices with their start and end apart: 61, of which 21 were waited for; matrix products, arithmetic and copies ran while one was open for 4% of the time, Pallas kernels for 32%

profile of v2, /device:TPU:97, one launch (start us, length us, event | category | flops | bytes accessed | tf_op | source)
XLA Modules:
  0.0 1114.8 jit_solution(1858484879508762564)
XLA Ops:
  18.4 63.0 %collective-permute-done = bf16[288,5120]{1,0:T(8,128)(2,1)S(1)} collective-permute-done((bf16[288,5120]{1,0:T(8,128)(2,1)}, bf16[288,5120]{1,0:T(8,128)(2,1)S(1)}, u32[]{:S(2)}, u32[]{:S(2)}) %collective-permute-start) | collective-permute-done | bytes 2949152 | tf_op jit(solution)/shard_map/ppermute | solution.py:249
  102.5 45.6 %collective-permute-done.29.len_ref = s32[3]{0:T(128)S(1)} collective-permute-done((s32[3]{0:T(128)S(1)}, s32[3]{0:T(128)S(1)}, u32[]{:S(2)}, u32[]{:S(2)}) %collective-permute-start.29) | collective-permute-done | bytes 44 | tf_op jit(solution)/shard_map/ppermute | solution.py:249
  163.1 22.0 %collective-permute-done.25.refs_4_ = bf16[640,1280]{1,0:T(8,128)(2,1)S(1)} collective-permute-done((bf16[640,1280]{1,0:T(8,128)(2,1)S(1)}, bf16[640,1280]{1,0:T(8,128)(2,1)S(1)}, u32[]{:S(2)}, u32[]{:S(2)}) %collective-permute-start.25) | collective-permute-done | bytes 1638432 | tf_op jit(solution)/shard_map/ppermute | solution.py:249
  193.3 26.9 %collective-permute-done.18.refs_4_ = bf16[640,1280]{1,0:T(8,128)(2,1)} collective-permute-done((bf16[640,1280]{1,0:T(8,128)(2,1)}, bf16[640,1280]{1,0:T(8,128)(2,1)}, u32[]{:S(2)}, u32[]{:S(2)}) %collective-permute-start.18) | collective-permute-done | bytes 1638432 | tf_op jit(solution)/shard_map/ppermute | solution.py:249
  225.5 19.2 %collective-permute-done.35.refs_6_ = bf16[640,896]{1,0:T(8,128)(2,1)} collective-permute-done((bf16[640,896]{1,0:T(8,128)(2,1)}, bf16[640,896]{1,0:T(8,128)(2,1)}, u32[]{:S(2)}, u32[]{:S(2)}) %collective-permute-start.35) | collective-permute-done | bytes 1146912 | tf_op jit(solution)/shard_map/ppermute | solution.py:249
  252.4 16.4 %norm.2.u_ref.u0 = bf16[1152,5120]{1,0:T(8,128)(2,1)} custom-call(bf16[1152,5120]{1,0:T(8,128)(2,1)} %bitcast.28, f32[1,5120]{1,0:T(1,128)} %bitcast.35), custom_call_target="tpu_custom_call" | custom-call | flops 47185920 | bytes 23592960 | tf_op jit(solution)/shard_map/norm/pallas_call | solution.py:36
  276.3 26.8 %qkv.2 = (bf16[2304,3200]{1,0:T(8,128)(2,1)}, bf16[1152,128]{1,0:T(8,128)(2,1)}, bf16[1152,128]{1,0:T(8,128)(2,1)}) custom-call(s32[1]{0:T(128)} %bitcast.4.dp_ref, s32[3]{0:T(128)} %len_ref.1, bf16[1152,5120]{1,0:T(8,128)(2,1)} %norm.2.u_ref.u0, f32[384,128]{1,0:T(8,128)} %get-tuple-element.78.cos_ref, f32[384,128]{1,0:T(8,128)} %get-tuple-element.79.sin_ref, ...), custom_call_target="tpu_custom_call" | custom-call | flops 21139292160 | bytes 20971520 | tf_op jit(solution)/shard_map/qkv/pallas_call | solution.py:101
  312.0 32.3 %collective-permute-done.4.refs_4_ = bf16[640,1280]{1,0:T(8,128)(2,1)} collective-permute-done((bf16[640,1280]{1,0:T(8,128)(2,1)S(1)}, bf16[640,1280]{1,0:T(8,128)(2,1)}, u32[]{:S(2)}, u32[]{:S(2)}) %collective-permute-start.4) | collective-permute-done | bytes 1638432 | tf_op jit(solution)/shard_map/ppermute | solution.py:249
  346.9 32.5 %collective-permute-done.27.refs_6_ = bf16[640,1280]{1,0:T(8,128)(2,1)} collective-permute-done((bf16[640,1280]{1,0:T(8,128)(2,1)}, bf16[640,1280]{1,0:T(8,128)(2,1)}, u32[]{:S(2)}, u32[]{:S(2)}) %collective-permute-start.27) | collective-permute-done | bytes 1638432 | tf_op jit(solution)/shard_map/ppermute | solution.py:249
  380.7 26.6 %qkv.3 = (bf16[2304,3200]{1,0:T(8,128)(2,1)}, bf16[1152,128]{1,0:T(8,128)(2,1)}, bf16[1152,128]{1,0:T(8,128)(2,1)}) custom-call(s32[1]{0:T(128)} %bitcast.4.dp_ref, s32[3]{0:T(128)} %copy-done.24, bf16[1152,5120]{1,0:T(8,128)(2,1)} %all-gather.2.cloned.1.call-done.u_ref.u1, f32[384,128]{1,0:T(8,128)} %get-tuple-element.78.cos_ref, ...), custom_call_target="tpu_custom_call", output_to_operand_aliasing={{0}: (13, {})} | custom-call | flops 21139292160 | bytes 20971520 | tf_op jit(solution)/shard_map/qkv/pallas_call | solution.py:101
  408.1 6.4 collective-permute-done.20.refs_6_
  418.3 38.9 %ffn.4.refs_8_ = bf16[2304,3200]{1,0:T(8,128)(2,1)} custom-call(s32[1]{0:T(128)} %bitcast.4.dp_ref, bf16[1152,5120]{1,0:T(8,128)(2,1)} %norm.2.u_ref.u0, bf16[1152,5120]{1,0:T(8,128)(2,1)} %all-gather.2.cloned.1.call-done.u_ref.u1, bf16[640,1280]{1,0:T(8,128)(2,1)} %copy-done.12, bf16[640,1280]{1,0:T(8,128)(2,1)} %copy-done.20, ...), custom_call_target="tpu_custom_call", output_to_operand_aliasing={{}: (11, {})} | custom-call | flops 30198988800 | bytes 36700160 | tf_op jit(solution)/shard_map/ffn/pallas_call | solution.py:156
  458.3 39.3 %ffn.5.refs_8_ = bf16[2304,3200]{1,0:T(8,128)(2,1)} custom-call(s32[1]{0:T(128)} %bitcast.4.dp_ref, bf16[1152,5120]{1,0:T(8,128)(2,1)} %norm.2.u_ref.u0, bf16[1152,5120]{1,0:T(8,128)(2,1)} %all-gather.2.cloned.1.call-done.u_ref.u1, bf16[640,1280]{1,0:T(8,128)(2,1)} %pad_maximum_fusion.6.refs_0_, ...), custom_call_target="tpu_custom_call", output_to_operand_aliasing={{}: (11, {})} | custom-call | flops 30198988800 | bytes 36700160 | tf_op jit(solution)/shard_map/ffn/pallas_call | solution.py:156
  499.0 38.9 %ffn.6.refs_8_ = bf16[2304,3200]{1,0:T(8,128)(2,1)} custom-call(s32[1]{0:T(128)} %bitcast.4.dp_ref, bf16[1152,5120]{1,0:T(8,128)(2,1)} %norm.2.u_ref.u0, bf16[1152,5120]{1,0:T(8,128)(2,1)} %all-gather.2.cloned.1.call-done.u_ref.u1, bf16[640,1280]{1,0:T(8,128)(2,1)} %pad_maximum_fusion.4.refs_0_, ...), custom_call_target="tpu_custom_call", output_to_operand_aliasing={{}: (11, {})} | custom-call | flops 30198988800 | bytes 36700160 | tf_op jit(solution)/shard_map/ffn/pallas_call | solution.py:156
  537.8 39.1 %ffn.7.x_ref = bf16[2304,3200]{1,0:T(8,128)(2,1)} custom-call(s32[1]{0:T(128)} %bitcast.4.dp_ref, bf16[1152,5120]{1,0:T(8,128)(2,1)} %norm.2.u_ref.u0, bf16[1152,5120]{1,0:T(8,128)(2,1)} %all-gather.2.cloned.1.call-done.u_ref.u1, bf16[640,1280]{1,0:T(8,128)(2,1)} %pad_maximum_fusion.2.refs_0_, ...), custom_call_target="tpu_custom_call", output_to_operand_aliasing={{}: (11, {})} | custom-call | flops 30198988800 | bytes 36700160 | tf_op jit(solution)/shard_map/ffn/pallas_call | solution.py:156
  576.9 17.1 %down.8.refs_0_ = bf16[2304,1280]{1,0:T(8,128)(2,1)} custom-call(s32[1]{0:T(128)} %bitcast.3.core_ref, bf16[2304,3200]{1,0:T(8,128)(2,1)} %ffn.7.x_ref, bf16[3200,640]{1,0:T(8,128)(2,1)} %pad_maximum_fusion.w0, bf16[3200,640]{1,0:T(8,128)(2,1)} %collective-permute-done.39.w1), custom_call_target="tpu_custom_call" | custom-call | flops 9437184000 | bytes 18513920 | tf_op jit(solution)/shard_map/down/pallas_call | solution.py:196
  594.1 17.3 %down.9 = bf16[2304,1280]{1,0:T(8,128)(2,1)} custom-call(s32[1]{0:T(128)} %bitcast.3.core_ref, bf16[2304,3200]{1,0:T(8,128)(2,1)} %ffn.7.x_ref, bf16[3200,640]{1,0:T(8,128)(2,1)} %collective-permute-done.37.w0, bf16[3200,640]{1,0:T(8,128)(2,1)} %collective-permute-done.38.w1, bf16[2304,1280]{1,0:T(8,128)(2,1)} %down.8.refs_0_), custom_call_target="tpu_custom_call", output_to_operand_aliasing={{}: (4, {})} | custom-call | flops 9437184000 | bytes 18513920 | tf_op jit(solution)/shard_map/down/pallas_call | solution.py:196
  614.3 17.3 %down.11 = bf16[1152,1280]{1,0:T(8,128)(2,1)} custom-call(s32[1]{0:T(128)} %bitcast.3.core_ref, bf16[2304,3200]{1,0:T(8,128)(2,1)} %ffn.7.x_ref, bf16[3200,640]{1,0:T(8,128)(2,1)} %pad_maximum_fusion.w0, bf16[3200,640]{1,0:T(8,128)(2,1)} %collective-permute-done.39.w1), custom_call_target="tpu_custom_call" | custom-call | flops 9437184000 | bytes 18513920 | tf_op jit(solution)/shard_map/down/pallas_call | solution.py:196
  631.7 71.1 %collective-permute-done.44.w0 = bf16[3200,640]{1,0:T(8,128)(2,1)} collective-permute-done((bf16[3200,640]{1,0:T(8,128)(2,1)}, bf16[3200,640]{1,0:T(8,128)(2,1)}, u32[]{:S(2)}, u32[]{:S(2)}) %collective-permute-start.44) | collective-permute-done | bytes 4096032 | tf_op jit(solution)/shard_map/ppermute | solution.py:249
  704.7 85.8 %collective-permute-done.42.w0 = bf16[3200,640]{1,0:T(8,128)(2,1)} collective-permute-done((bf16[3200,640]{1,0:T(8,128)(2,1)}, bf16[3200,640]{1,0:T(8,128)(2,1)}, u32[]{:S(2)}, u32[]{:S(2)}) %collective-permute-start.42) | collective-permute-done | bytes 4096032 | tf_op jit(solution)/shard_map/ppermute | solution.py:249
  791.8 17.1 %down.10 = bf16[1152,1280]{1,0:T(8,128)(2,1)} custom-call(s32[1]{0:T(128)} %bitcast.3.core_ref, bf16[2304,3200]{1,0:T(8,128)(2,1)} %ffn.7.x_ref, bf16[3200,640]{1,0:T(8,128)(2,1)} %collective-permute-done.37.w0, bf16[3200,640]{1,0:T(8,128)(2,1)} %collective-permute-done.38.w1), custom_call_target="tpu_custom_call" | custom-call | flops 9437184000 | bytes 18513920 | tf_op jit(solution)/shard_map/down/pallas_call | solution.py:196
  813.2 17.3 %down.15 = bf16[1152,1280]{1,0:T(8,128)(2,1)} custom-call(s32[1]{0:T(128)} %bitcast.3.core_ref, bf16[2304,3200]{1,0:T(8,128)(2,1)} %ffn.7.x_ref, bf16[3200,640]{1,0:T(8,128)(2,1)} %collective-permute-done.44.w0, bf16[3200,640]{1,0:T(8,128)(2,1)} %collective-permute-done.45.w1), custom_call_target="tpu_custom_call" | custom-call | flops 9437184000 | bytes 18513920 | tf_op jit(solution)/shard_map/down/pallas_call | solution.py:196
  830.7 17.2 %down.14 = bf16[1152,1280]{1,0:T(8,128)(2,1)} custom-call(s32[1]{0:T(128)} %bitcast.3.core_ref, bf16[2304,3200]{1,0:T(8,128)(2,1)} %ffn.7.x_ref, bf16[3200,640]{1,0:T(8,128)(2,1)} %collective-permute-done.42.w0, bf16[3200,640]{1,0:T(8,128)(2,1)} %collective-permute-done.43.w1), custom_call_target="tpu_custom_call" | custom-call | flops 9437184000 | bytes 18513920 | tf_op jit(solution)/shard_map/down/pallas_call | solution.py:196
  847.9 48.4 %collective-permute-done.47 = bf16[1152,1280]{1,0:T(8,128)(2,1)S(1)} collective-permute-done((bf16[1152,1280]{1,0:T(8,128)(2,1)}, bf16[1152,1280]{1,0:T(8,128)(2,1)S(1)}, u32[]{:S(2)}, u32[]{:S(2)}) %collective-permute-start.47) | collective-permute-done | bytes 2949152 | tf_op jit(solution)/shard_map/ppermute | solution.py:249
  900.6 17.4 %down.12.refs_0_ = bf16[2304,1280]{1,0:T(8,128)(2,1)} custom-call(s32[1]{0:T(128)} %bitcast.3.core_ref, bf16[2304,3200]{1,0:T(8,128)(2,1)} %ffn.7.x_ref, bf16[3200,640]{1,0:T(8,128)(2,1)} %collective-permute-done.44.w0, bf16[3200,640]{1,0:T(8,128)(2,1)} %collective-permute-done.45.w1), custom_call_target="tpu_custom_call" | custom-call | flops 9437184000 | bytes 18513920 | tf_op jit(solution)/shard_map/down/pallas_call | solution.py:196
  918.0 17.2 %down.13 = bf16[2304,1280]{1,0:T(8,128)(2,1)} custom-call(s32[1]{0:T(128)} %bitcast.3.core_ref, bf16[2304,3200]{1,0:T(8,128)(2,1)} %ffn.7.x_ref, bf16[3200,640]{1,0:T(8,128)(2,1)} %collective-permute-done.42.w0, bf16[3200,640]{1,0:T(8,128)(2,1)} %collective-permute-done.43.w1, bf16[2304,1280]{1,0:T(8,128)(2,1)} %down.12.refs_0_), custom_call_target="tpu_custom_call", output_to_operand_aliasing={{}: (4, {})} | custom-call | flops 9437184000 | bytes 18513920 | tf_op jit(solution)/shard_map/down/pallas_call | solution.py:196
  941.4 57.1 %reduce-scatter.9.cloned.1.call-done = bf16[2,288,1280]{2,1,0:T(8,128)(2,1)} async-done(((bf16[2,1152,1280]{2,1,0:T(8,128)(2,1)}), bf16[2,288,1280]{2,1,0:T(8,128)(2,1)}) %reduce-scatter.9.cloned.1.call-update) | async-done | bytes 1474576 | tf_op jit(solution)/shard_map/reduce_scatter | solution.py:326
  1006.5 10.7 collective-permute-done.46
  1019.6 18.3 %collective-permute-done.52.refs_1_ = bf16[288,2560]{1,0:T(8,128)(2,1)S(1)} collective-permute-done((bf16[288,2560]{1,0:T(8,128)(2,1)S(1)}, bf16[288,2560]{1,0:T(8,128)(2,1)S(1)}, u32[]{:S(2)}, u32[]{:S(2)}) %collective-permute-start.52) | collective-permute-done | bytes 1474592 | tf_op jit(solution)/shard_map/ppermute | solution.py:252
  1039.3 30.2 %collective-permute-done.48.refs_1_ = bf16[288,2560]{1,0:T(8,128)(2,1)S(1)} collective-permute-done((bf16[288,2560]{1,0:T(8,128)(2,1)S(1)}, bf16[288,2560]{1,0:T(8,128)(2,1)S(1)}, u32[]{:S(2)}, u32[]{:S(2)}) %collective-permute-start.48) | collective-permute-done | bytes 1474592 | tf_op jit(solution)/shard_map/ppermute | solution.py:252
  1073.0 13.6 %collective-permute-done.54.refs_3_ = bf16[288,1280]{1,0:T(8,128)(2,1)} collective-permute-done((bf16[288,1280]{1,0:T(8,128)(2,1)S(1)}, bf16[288,1280]{1,0:T(8,128)(2,1)}, u32[]{:S(2)}, u32[]{:S(2)}) %collective-permute-start.54) | collective-permute-done | bytes 737312 | tf_op jit(solution)/shard_map/ppermute | solution.py:252
  1091.9 10.5 collective-permute-done.50.refs_3_
  (201 shorter events, 142.3 us)
Async XLA Ops:
  7.2 373.5 %all-gather.2.cloned.1.call-start = ((), (), s32[]{:S(2)}) async-start(), calls=%async_computation.4 | async-start | bytes 14745600 | tf_op jit(solution)/shard_map/all_gather | solution.py:296
  16.2 65.1 %collective-permute-start = (bf16[288,5120]{1,0:T(8,128)(2,1)}, bf16[288,5120]{1,0:T(8,128)(2,1)S(1)}, u32[]{:S(2)}, u32[]{:S(2)}) collective-permute-start(bf16[288,5120]{1,0:T(8,128)(2,1)} %norm.3), channel_id=1, source_target_pairs={{0,2},{1,3},{2,0},{3,1},{4,6},{5,7},{6,4},{7,5},{8,10},{9,11},{10,... | collective-permute-start | bytes 8847368 | tf_op jit(solution)/shard_map/ppermute | solution.py:249
  83.0 852.3 %reduce-scatter.5.cloned.1.call-start = ((), (), s32[]{:S(2)}) async-start(), calls=%async_computation.5 | async-start | bytes 7372800 | tf_op jit(solution)/shard_map/reduce_scatter | solution.py:326
  86.7 64.3 %collective-permute-start.31 = (bf16[640,896]{1,0:T(8,128)(2,1)S(1)}, bf16[640,896]{1,0:T(8,128)(2,1)}, u32[]{:S(2)}, u32[]{:S(2)}) collective-permute-start(bf16[640,896]{1,0:T(8,128)(2,1)S(1)} %get-tuple-element.31), channel_id=1, source_target_pairs={{0,2},{1,3},{2,0},{3,1},{4,6},{5,7},{6,4},{7,5},{8,10},{9,11},{10,... | collective-permute-start | bytes 3440648 | tf_op jit(solution)/shard_map/ppermute | solution.py:249
  95.1 61.7 %collective-permute-start.23 = (bf16[640,1280]{1,0:T(8,128)(2,1)S(1)}, bf16[640,1280]{1,0:T(8,128)(2,1)S(1)}, u32[]{:S(2)}, u32[]{:S(2)}) collective-permute-start(bf16[640,1280]{1,0:T(8,128)(2,1)S(1)} %pad_maximum_fusion.9), channel_id=1, source_target_pairs={{0,2},{1,3},{2,0},{3,1},{4,6},{5,7},{6,4},{7,5},{8,10},{9,11},{10,... | collective-permute-start | bytes 4915208 | tf_op jit(solution)/shard_map/ppermute | solution.py:249
  95.3 59.7 %collective-permute-start.33 = (bf16[640,896]{1,0:T(8,128)(2,1)S(1)}, bf16[640,896]{1,0:T(8,128)(2,1)}, u32[]{:S(2)}, u32[]{:S(2)}) collective-permute-start(bf16[640,896]{1,0:T(8,128)(2,1)S(1)} %get-tuple-element.30.refs_0_), channel_id=1, source_target_pairs={{0,6},{1,7},{2,4},{3,5},{4,2},{5,3},{6,0},{7,1},{8,14},{9,15},{10,... | collective-permute-start | bytes 3440648 | tf_op jit(solution)/shard_map/ppermute | solution.py:249
  98.2 56.8 %collective-permute-start.30 = (bf16[640,896]{1,0:T(8,128)(2,1)S(1)}, bf16[640,896]{1,0:T(8,128)(2,1)S(1)}, u32[]{:S(2)}, u32[]{:S(2)}) collective-permute-start(bf16[640,896]{1,0:T(8,128)(2,1)S(1)} %get-tuple-element.30.refs_0_), channel_id=1, source_target_pairs={{0,1},{1,0},{2,3},{3,2},{4,5},{5,4},{6,7},{7,6},{8,9},{9,8},{10,11... | collective-permute-start | bytes 3440648 | tf_op jit(solution)/shard_map/ppermute | solution.py:249
  155.0 65.2 %collective-permute-start.18 = (bf16[640,1280]{1,0:T(8,128)(2,1)}, bf16[640,1280]{1,0:T(8,128)(2,1)}, u32[]{:S(2)}, u32[]{:S(2)}) collective-permute-start(bf16[640,1280]{1,0:T(8,128)(2,1)} %pad_maximum_fusion.6.refs_0_), channel_id=1, source_target_pairs={{0,6},{1,7},{2,4},{3,5},{4,2},{5,3},{6,0},{7,1},{8,14},{9,15},{10,... | collective-permute-start | bytes 4915208 | tf_op jit(solution)/shard_map/ppermute | solution.py:249
  157.9 86.8 %collective-permute-start.35 = (bf16[640,896]{1,0:T(8,128)(2,1)}, bf16[640,896]{1,0:T(8,128)(2,1)}, u32[]{:S(2)}, u32[]{:S(2)}) collective-permute-start(bf16[640,896]{1,0:T(8,128)(2,1)} %collective-permute-done.31.refs_2_), channel_id=1, source_target_pairs={{0,6},{1,7},{2,4},{3,5},{4,2},{5,3},{6,0},{7,1},{8,14},{9,15},{10,... | collective-permute-start | bytes 3440648 | tf_op jit(solution)/shard_map/ppermute | solution.py:249
  185.0 85.5 %collective-permute-start.15 = (bf16[640,1280]{1,0:T(8,128)(2,1)}, bf16[640,1280]{1,0:T(8,128)(2,1)}, u32[]{:S(2)}, u32[]{:S(2)}) collective-permute-start(bf16[640,1280]{1,0:T(8,128)(2,1)} %pad_maximum_fusion.6.refs_0_), channel_id=1, source_target_pairs={{0,1},{1,0},{2,3},{3,2},{4,5},{5,4},{6,7},{7,6},{8,9},{9,8},{10,11... | collective-permute-start | bytes 4915208 | tf_op jit(solution)/shard_map/ppermute | solution.py:249
  190.3 82.9 %collective-permute-start.9 = (bf16[640,1280]{1,0:T(8,128)(2,1)}, bf16[640,1280]{1,0:T(8,128)(2,1)}, u32[]{:S(2)}, u32[]{:S(2)}) collective-permute-start(bf16[640,1280]{1,0:T(8,128)(2,1)} %pad_maximum_fusion.5), channel_id=1, source_target_pairs={{0,2},{1,3},{2,0},{3,1},{4,6},{5,7},{6,4},{7,5},{8,10},{9,11},{10,... | collective-permute-start | bytes 4915208 | tf_op jit(solution)/shard_map/ppermute | solution.py:249
  192.4 81.1 %collective-permute-start.32 = (bf16[640,896]{1,0:T(8,128)(2,1)}, bf16[640,896]{1,0:T(8,128)(2,1)}, u32[]{:S(2)}, u32[]{:S(2)}) collective-permute-start(bf16[640,896]{1,0:T(8,128)(2,1)} %collective-permute-done.31.refs_2_), channel_id=1, source_target_pairs={{0,1},{1,0},{2,3},{3,2},{4,5},{5,4},{6,7},{7,6},{8,9},{9,8},{10,11... | collective-permute-start | bytes 3440648 | tf_op jit(solution)/shard_map/ppermute | solution.py:249
  220.1 53.3 %collective-permute-start.34 = (bf16[640,896]{1,0:T(8,128)(2,1)}, bf16[640,896]{1,0:T(8,128)(2,1)}, u32[]{:S(2)}, u32[]{:S(2)}) collective-permute-start(bf16[640,896]{1,0:T(8,128)(2,1)} %collective-permute-done.33.refs_4_), channel_id=1, source_target_pairs={{0,1},{1,0},{2,3},{3,2},{4,5},{5,4},{6,7},{7,6},{8,9},{9,8},{10,11... | collective-permute-start | bytes 3440648 | tf_op jit(solution)/shard_map/ppermute | solution.py:249
  273.5 70.8 %collective-permute-start.4 = (bf16[640,1280]{1,0:T(8,128)(2,1)S(1)}, bf16[640,1280]{1,0:T(8,128)(2,1)}, u32[]{:S(2)}, u32[]{:S(2)}) collective-permute-start(bf16[640,1280]{1,0:T(8,128)(2,1)S(1)} %copy-done.13), channel_id=1, source_target_pairs={{0,6},{1,7},{2,4},{3,5},{4,2},{5,3},{6,0},{7,1},{8,14},{9,15},{10,... | collective-permute-start | bytes 4915208 | tf_op jit(solution)/shard_map/ppermute | solution.py:249
  273.6 105.8 %collective-permute-start.27 = (bf16[640,1280]{1,0:T(8,128)(2,1)}, bf16[640,1280]{1,0:T(8,128)(2,1)}, u32[]{:S(2)}, u32[]{:S(2)}) collective-permute-start(bf16[640,1280]{1,0:T(8,128)(2,1)} %copy-done.18), channel_id=1, source_target_pairs={{0,6},{1,7},{2,4},{3,5},{4,2},{5,3},{6,0},{7,1},{8,14},{9,15},{10,... | collective-permute-start | bytes 4915208 | tf_op jit(solution)/shard_map/ppermute | solution.py:249
  309.2 98.1 %collective-permute-start.1 = (bf16[640,1280]{1,0:T(8,128)(2,1)S(1)}, bf16[640,1280]{1,0:T(8,128)(2,1)}, u32[]{:S(2)}, u32[]{:S(2)}) collective-permute-start(bf16[640,1280]{1,0:T(8,128)(2,1)S(1)} %copy-done.13), channel_id=1, source_target_pairs={{0,1},{1,0},{2,3},{3,2},{4,5},{5,4},{6,7},{7,6},{8,9},{9,8},{10,11... | collective-permute-start | bytes 4915208 | tf_op jit(solution)/shard_map/ppermute | solution.py:249
  310.5 97.0 %collective-permute-start.24 = (bf16[640,1280]{1,0:T(8,128)(2,1)}, bf16[640,1280]{1,0:T(8,128)(2,1)S(1)}, u32[]{:S(2)}, u32[]{:S(2)}) collective-permute-start(bf16[640,1280]{1,0:T(8,128)(2,1)} %copy-done.18), channel_id=1, source_target_pairs={{0,1},{1,0},{2,3},{3,2},{4,5},{5,4},{6,7},{7,6},{8,9},{9,8},{10,11... | collective-permute-start | bytes 4915208 | tf_op jit(solution)/shard_map/ppermute | solution.py:249
  310.9 96.7 %collective-permute-start.26 = (bf16[640,1280]{1,0:T(8,128)(2,1)}, bf16[640,1280]{1,0:T(8,128)(2,1)}, u32[]{:S(2)}, u32[]{:S(2)}) collective-permute-start(bf16[640,1280]{1,0:T(8,128)(2,1)} %copy-done.19), channel_id=1, source_target_pairs={{0,1},{1,0},{2,3},{3,2},{4,5},{5,4},{6,7},{7,6},{8,9},{9,8},{10,11... | collective-permute-start | bytes 4915208 | tf_op jit(solution)/shard_map/ppermute | solution.py:249
  344.3 70.2 %collective-permute-start.20 = (bf16[640,1280]{1,0:T(8,128)(2,1)}, bf16[640,1280]{1,0:T(8,128)(2,1)}, u32[]{:S(2)}, u32[]{:S(2)}) collective-permute-start(bf16[640,1280]{1,0:T(8,128)(2,1)} %collective-permute-done.16.refs_2_), channel_id=1, source_target_pairs={{0,6},{1,7},{2,4},{3,5},{4,2},{5,3},{6,0},{7,1},{8,14},{9,15},{10,... | collective-permute-start | bytes 4915208 | tf_op jit(solution)/shard_map/ppermute | solution.py:249
  407.3 91.1 %collective-permute-start.37 = (bf16[3200,640]{1,0:T(8,128)(2,1)}, bf16[3200,640]{1,0:T(8,128)(2,1)}, u32[]{:S(2)}, u32[]{:S(2)}) collective-permute-start(bf16[3200,640]{1,0:T(8,128)(2,1)} %pad_maximum_fusion.1), channel_id=1, source_target_pairs={{0,2},{1,3},{2,0},{3,1},{4,6},{5,7},{6,4},{7,5},{8,10},{9,11},{10,... | collective-permute-start | bytes 12288008 | tf_op jit(solution)/shard_map/ppermute | solution.py:249
  497.6 79.3 %collective-permute-start.39 = (bf16[3200,640]{1,0:T(8,128)(2,1)S(1)}, bf16[3200,640]{1,0:T(8,128)(2,1)}, u32[]{:S(2)}, u32[]{:S(2)}) collective-permute-start(bf16[3200,640]{1,0:T(8,128)(2,1)S(1)} %copy-done.4), channel_id=1, source_target_pairs={{0,1},{1,0},{2,3},{3,2},{4,5},{5,4},{6,7},{7,6},{8,9},{9,8},{10,11... | collective-permute-start | bytes 12288008 | tf_op jit(solution)/shard_map/ppermute | solution.py:249
  498.8 95.3 %collective-permute-start.38 = (bf16[3200,640]{1,0:T(8,128)(2,1)}, bf16[3200,640]{1,0:T(8,128)(2,1)}, u32[]{:S(2)}, u32[]{:S(2)}) collective-permute-start(bf16[3200,640]{1,0:T(8,128)(2,1)} %collective-permute-done.37.w0), channel_id=1, source_target_pairs={{0,1},{1,0},{2,3},{3,2},{4,5},{5,4},{6,7},{7,6},{8,9},{9,8},{10,11... | collective-permute-start | bytes 12288008 | tf_op jit(solution)/shard_map/ppermute | solution.py:249
  611.4 326.3 %reduce-scatter.7.cloned.1.call-start = ((), (), s32[]{:S(2)}) async-start(), calls=%async_computation.6 | async-start | bytes 3686400 | tf_op jit(solution)/shard_map/reduce_scatter | solution.py:329
  611.5 91.3 %collective-permute-start.44 = (bf16[3200,640]{1,0:T(8,128)(2,1)}, bf16[3200,640]{1,0:T(8,128)(2,1)}, u32[]{:S(2)}, u32[]{:S(2)}) collective-permute-start(bf16[3200,640]{1,0:T(8,128)(2,1)} %pad_maximum_fusion.w0), channel_id=1, source_target_pairs={{0,6},{1,7},{2,4},{3,5},{4,2},{5,3},{6,0},{7,1},{8,14},{9,15},{10,... | collective-permute-start | bytes 12288008 | tf_op jit(solution)/shard_map/ppermute | solution.py:249
  614.2 176.4 %collective-permute-start.42 = (bf16[3200,640]{1,0:T(8,128)(2,1)}, bf16[3200,640]{1,0:T(8,128)(2,1)}, u32[]{:S(2)}, u32[]{:S(2)}) collective-permute-start(bf16[3200,640]{1,0:T(8,128)(2,1)} %collective-permute-done.37.w0), channel_id=1, source_target_pairs={{0,6},{1,7},{2,4},{3,5},{4,2},{5,3},{6,0},{7,1},{8,14},{9,15},{10,... | collective-permute-start | bytes 12288008 | tf_op jit(solution)/shard_map/ppermute | solution.py:249
  631.6 177.3 %collective-permute-start.41 = (bf16[1152,1280]{1,0:T(8,128)(2,1)}, bf16[1152,1280]{1,0:T(8,128)(2,1)S(1)}, u32[]{:S(2)}, u32[]{:S(2)}) collective-permute-start(bf16[1152,1280]{1,0:T(8,128)(2,1)} %down.11), channel_id=1, source_target_pairs={{0,2},{1,3},{2,0},{3,1},{4,6},{5,7},{6,4},{7,5},{8,10},{9,11},{10,... | collective-permute-start | bytes 8847368 | tf_op jit(solution)/shard_map/ppermute | solution.py:249
  702.8 110.4 %collective-permute-start.45 = (bf16[3200,640]{1,0:T(8,128)(2,1)}, bf16[3200,640]{1,0:T(8,128)(2,1)}, u32[]{:S(2)}, u32[]{:S(2)}) collective-permute-start(bf16[3200,640]{1,0:T(8,128)(2,1)} %collective-permute-done.44.w0), channel_id=1, source_target_pairs={{0,1},{1,0},{2,3},{3,2},{4,5},{5,4},{6,7},{7,6},{8,9},{9,8},{10,11... | collective-permute-start | bytes 12288008 | tf_op jit(solution)/shard_map/ppermute | solution.py:249
  813.1 127.1 %reduce-scatter.11.cloned.1.call-start = ((), (), s32[]{:S(2)}) async-start(), calls=%async_computation.8 | async-start | bytes 3686400 | tf_op jit(solution)/shard_map/reduce_scatter | solution.py:329
  830.6 65.8 %collective-permute-start.47 = (bf16[1152,1280]{1,0:T(8,128)(2,1)}, bf16[1152,1280]{1,0:T(8,128)(2,1)S(1)}, u32[]{:S(2)}, u32[]{:S(2)}) collective-permute-start(bf16[1152,1280]{1,0:T(8,128)(2,1)} %down.15), channel_id=1, source_target_pairs={{0,2},{1,3},{2,0},{3,1},{4,6},{5,7},{6,4},{7,5},{8,10},{9,11},{10,... | collective-permute-start | bytes 8847368 | tf_op jit(solution)/shard_map/ppermute | solution.py:249
  900.5 98.0 %reduce-scatter.9.cloned.1.call-start = ((), (), s32[]{:S(2)}) async-start(), calls=%async_computation.7 | async-start | bytes 7372800 | tf_op jit(solution)/shard_map/reduce_scatter | solution.py:326
  937.3 63.7 %collective-permute-start.40 = (bf16[288,1280]{1,0:T(8,128)(2,1)}, bf16[288,1280]{1,0:T(8,128)(2,1)}, u32[]{:S(2)}, u32[]{:S(2)}) collective-permute-start(bf16[288,1280]{1,0:T(8,128)(2,1)} %slice_bitcast_fusion.2), channel_id=1, source_target_pairs={{0,2},{1,3},{2,0},{3,1},{4,6},{5,7},{6,4},{7,5},{8,10},{9,11},{10,... | collective-permute-start | bytes 2211848 | tf_op jit(solution)/shard_map/ppermute | solution.py:249
  1018.1 52.9 %collective-permute-start.49 = (bf16[288,2560]{1,0:T(8,128)(2,1)S(1)}, bf16[288,2560]{1,0:T(8,128)(2,1)S(1)}, u32[]{:S(2)}, u32[]{:S(2)}) collective-permute-start(bf16[288,2560]{1,0:T(8,128)(2,1)S(1)} %fusion.3.refs_0_), channel_id=1, source_target_pairs={{0,24},{8,16},{16,8},{24,0},{1,25},{9,17},{17,9},{25,1},{2,26},{10... | collective-permute-start | bytes 4423688 | tf_op jit(solution)/shard_map/ppermute | solution.py:252
  (56 other events, 1713.0 us)
Sparse Core Ops, SparseCore 0:
  83.1 113.8 all-gather.1
  611.5 60.6 reduce-scatter.4
  813.2 36.3 reduce-scatter.6
  900.6 37.0 reduce-scatter.10
  940.5 57.9 reduce-scatter.8
